TPU v7x, 32 devices: a whole 2x2x4 slice. The times are simulated.
32 devices in a mesh: dp: 4 (over z), expert: 8 (over y, x, core).
Axes of the slice: x: 2, y: 2, z: 4, core: 2. Of those that a mesh axis runs over, the one named last changes fastest.
Arguments:
- tokens: bfloat16 [2048, 2048], P(('dp', 'expert')), may hold values from -6 to 6
- norm_gain: bfloat16 [2048], replicated, may hold values from 0.099609375 to 1.8984375
- router_weight: bfloat16 [2048, 8], replicated, may hold values from -0.125 to 0.125
- gate_weight: bfloat16 [8, 2048, 5120], P('expert', None, 'dp'), may hold values from -0.125 to 0.125
- up_weight: bfloat16 [8, 2048, 5120], P('expert', None, 'dp'), may hold values from -0.125 to 0.125
- down_weight: bfloat16 [8, 5120, 2048], P('expert', 'dp'), may hold values from -0.078125 to 0.078125
- expert_picks: int32 [4, 8, 128], P('dp'), may hold values from 0 to 511, as said below
- final_gain: bfloat16 [2048], replicated, may hold values from 0.099609375 to 1.8984375
- kv_weight: bfloat16 [2048, 8, 6, 2, 64], P(None, 'expert'), may hold values from -0.125 to 0.125
Outputs:
- moe_out: bfloat16 [2048, 2048], P(('dp', 'expert'))
- kv_cache: bfloat16 [2048, 8, 6, 2, 64], P('dp', 'expert')
Inputs may be any that keep to these rules, and one draw needn't show every extreme that they name: `expert_picks`: for each group and expert, 128 different positions in the group. Of the 64 tokens of one device (positions s * 64 to (s + 1) * 64 - 1) one expert picks at most 32, and for every group and expert some device's tokens are picked exactly 32 times.
All inputs are finite; a program needn't handle non-finite values.
Results may differ from a plain program's by a relative error of at most 0.013.
Values may be sent and summed in bfloat16 or wider, within the bound.
No kernel may reach another device: no remote copies, remote signals or barrier semaphores. Data moves between devices by JAX's collectives and lax.ppermute only.
A program may use at most 128 MiB of HBM per device.

v0:
```python
import functools

import jax
import jax.numpy as jnp
from jax import lax
from jax.experimental import pallas as pl
from jax.experimental.pallas import tpu as pltpu
from jax.sharding import PartitionSpec as P


def shuffle(value, axis, mask):
    size = lax.axis_size(axis)
    return lax.ppermute(value, axis, [(i, i ^ mask) for i in range(size)])


def plane_gather(value):
    size = lax.axis_size("expert")
    blocks = {0: value}
    for mask in range(2, size, 2):
        blocks[mask] = shuffle(value, "expert", mask)
    for mask in range(0, size, 2):
        blocks[mask + 1] = shuffle(blocks[mask], "expert", 1)
    return [blocks[mask] for mask in range(size)]


def select_body(base_ref, picks_ref, gain_ref, *refs):
    blocks, out_ref = refs[:-1], refs[-1]
    rows = blocks[0].shape[0]
    capacity = picks_ref.shape[1]
    column = lax.broadcasted_iota(jnp.int32, (rows, capacity), 0)
    hits = jnp.concatenate(
        [
            (column + base_ref[k] == picks_ref[...]).astype(jnp.bfloat16)
            for k in range(len(blocks))
        ],
        axis=0,
    )
    values = jnp.concatenate([block[...] for block in blocks], axis=0)
    chosen = lax.dot_general(
        hits, values, (((0,), (0,)), ((), ())), preferred_element_type=jnp.float32
    )
    scale = lax.rsqrt(jnp.mean(chosen * chosen, axis=-1, keepdims=True) + 1e-06)
    gain = gain_ref[...].astype(jnp.float32)
    out_ref[...] = (chosen * scale * gain).astype(out_ref.dtype)


def fits(blocks):
    return len(blocks) * blocks[0].size <= 2 * 1024 * 1024


def plain_normalize(wide, gain):
    scale = lax.rsqrt(jnp.mean(wide * wide, axis=-1, keepdims=True) + 1e-06)
    return (wide * scale * gain.astype(jnp.float32)).astype(jnp.bfloat16)


def token_ids(base, rows):
    return (base[:, None] + jnp.arange(rows, dtype=jnp.int32)[None, :]).reshape(-1)


def plain_select(blocks, picks, base, gain):
    ids = token_ids(base, blocks[0].shape[0])
    hits = (picks.reshape(-1, 1) == ids[None, :]).astype(jnp.bfloat16)
    values = jnp.concatenate(blocks, axis=0)
    return plain_normalize(jnp.dot(hits, values, preferred_element_type=jnp.float32), gain)


def plain_prepare(blocks, picks, base, gain, router):
    rows = blocks[0].shape[0]
    all_ids = jnp.arange(len(blocks) * rows, dtype=jnp.int32)
    place = (all_ids[:, None] == token_ids(base, rows)[None, :]).astype(jnp.bfloat16)
    values = jnp.concatenate(blocks, axis=0)
    here = jnp.dot(place, values, preferred_element_type=jnp.float32)
    probs = jax.nn.sigmoid(
        jnp.dot(plain_normalize(here, gain), router, preferred_element_type=jnp.float32)
    )
    hits = all_ids[:, None, None] == picks[None, :, :]
    combine = jnp.where(hits, probs[:, :, None], 0.0).astype(jnp.bfloat16)
    return combine.reshape(all_ids.shape[0], -1), here.astype(jnp.bfloat16)


def plain_finish(blocks, combine, here, own, gain, kv_matrix, rows):
    outputs = jnp.concatenate(blocks, axis=0)
    added = jnp.dot(combine, outputs, preferred_element_type=jnp.float32)
    moe = (here.astype(jnp.float32) + added).astype(jnp.bfloat16)
    encoded = plain_normalize(moe.astype(jnp.float32), gain)
    cache = lax.dot_general(
        kv_matrix, encoded, (((1,), (1,)), ((), ())), preferred_element_type=jnp.float32
    ).astype(jnp.bfloat16)
    return lax.dynamic_slice_in_dim(moe, own * rows, rows, 0), cache


def select(blocks, picks, base, gain):
    if not fits(blocks):
        return plain_select(blocks, picks, base, gain)
    capacity, width = picks.shape[-1], blocks[0].shape[1]
    vmem = pl.BlockSpec(memory_space=pltpu.VMEM)
    return pl.pallas_call(
        select_body,
        in_specs=[pl.BlockSpec(memory_space=pltpu.SMEM)] + [vmem] * (2 + len(blocks)),
        out_specs=vmem,
        out_shape=jax.ShapeDtypeStruct((capacity, width), jnp.bfloat16),
        compiler_params=pltpu.CompilerParams(vmem_limit_bytes=48 * 1024 * 1024),
        name="select",
    )(base, picks.reshape(1, capacity), gain.reshape(1, width), *blocks)


def prepare_body(base_ref, own_ref, picks_ref, gain_ref, router_ref, *refs):
    blocks, (combine_ref, here_ref) = refs[:-2], refs[-2:]
    rows, _ = blocks[0].shape
    shards = len(blocks)
    capacity = picks_ref.shape[1]
    gain = gain_ref[...].astype(jnp.float32)
    for k in range(shards):
        wide = blocks[k][...].astype(jnp.float32)
        scale = lax.rsqrt(jnp.mean(wide * wide, axis=-1, keepdims=True) + 1e-06)
        normed = (wide * scale * gain).astype(jnp.bfloat16)
        logits = jnp.dot(normed, router_ref[...], preferred_element_type=jnp.float32)
        probs = jax.nn.sigmoid(logits)
        start = pl.multiple_of(base_ref[k], rows)
        here_ref[pl.ds(start, rows), :] = blocks[k][...]
        ids = lax.broadcasted_iota(jnp.int32, (rows, capacity), 0) + start
        for j in range(shards):
            hit = ids == picks_ref[j : j + 1, :]
            combine_ref[pl.ds(start, rows), j * capacity : (j + 1) * capacity] = (
                jnp.where(hit, probs[:, j : j + 1], 0.0).astype(jnp.bfloat16)
            )


def prepare(blocks, picks, base, own, gain, router):
    if not fits(blocks):
        return plain_prepare(blocks, picks, base, gain, router)
    shards, (rows, width) = len(blocks), blocks[0].shape
    capacity = picks.shape[1]
    vmem = pl.BlockSpec(memory_space=pltpu.VMEM)
    smem = pl.BlockSpec(memory_space=pltpu.SMEM)
    return pl.pallas_call(
        prepare_body,
        in_specs=[smem, smem] + [vmem] * (3 + shards),
        out_specs=[vmem, vmem],
        out_shape=[
            jax.ShapeDtypeStruct((shards * rows, shards * capacity), jnp.bfloat16),
            jax.ShapeDtypeStruct((shards * rows, width), jnp.bfloat16),
        ],
        compiler_params=pltpu.CompilerParams(vmem_limit_bytes=56 * 1024 * 1024),
        name="prepare",
    )(base, own.reshape(1), picks, gain.reshape(1, width), router, *blocks)


def finish_body(stage, stages, shards, *refs):
    own_ref, combine_hbm, here_hbm, gain_ref, kv_hbm = refs[:5]
    blocks, refs = refs[5 : 5 + shards], refs[5 + shards :]
    first, last = stage == 0, stage == stages - 1
    if not first:
        (square_hbm, cache_hbm, *before), refs = refs[: 2 + stage], refs[2 + stage :]
    outs, (combine_ref, here_ref, kv_ref, output_ref, square_ref, cache_ref, sem) = (
        refs[:-7],
        refs[-7:],
    )
    capacity, piece = blocks[0].shape
    span = slice(stage * piece, (stage + 1) * piece)
    copies = [pltpu.make_async_copy(combine_hbm, combine_ref, sem.at[0])]
    for k in range(shards):
        place = output_ref.at[k * capacity : (k + 1) * capacity, :]
        copies.append(pltpu.make_async_copy(blocks[k], place, sem.at[1 + k]))
    copies.append(
        pltpu.make_async_copy(here_hbm.at[:, span], here_ref, sem.at[shards + 1])
    )
    late = [pltpu.make_async_copy(kv_hbm.at[:, span], kv_ref, sem.at[shards + 2])]
    if not first:
        late.append(pltpu.make_async_copy(square_hbm, square_ref, sem.at[shards + 3]))
        late.append(pltpu.make_async_copy(cache_hbm, cache_ref, sem.at[shards + 4]))
    for copy in copies + late:
        copy.start()
    for copy in copies:
        copy.wait()
    added = jnp.dot(combine_ref[...], output_ref[...], preferred_element_type=jnp.float32)
    here_ref[...] = (here_ref[...].astype(jnp.float32) + added).astype(jnp.bfloat16)
    rows = outs[0].shape[0]
    mine = here_ref[pl.ds(pl.multiple_of(own_ref[0] * rows, rows), rows), :]
    if last:
        for j in range(stage):
            outs[0][:, j * piece : (j + 1) * piece] = before[j][...]
        outs[0][:, span] = mine
    else:
        outs[0][...] = mine
    wide = here_ref[...].astype(jnp.float32)
    scaled = (wide * gain_ref[:, span].astype(jnp.float32)).astype(jnp.bfloat16)
    square = jnp.sum(wide * wide, axis=-1, keepdims=True)
    for copy in late:
        copy.wait()
    cache = lax.dot_general(
        kv_ref[...], scaled, (((1,), (1,)), ((), ())), preferred_element_type=jnp.float32
    )
    if not first:
        cache = cache + cache_ref[...]
        square = square + square_ref[...]
    square = jnp.broadcast_to(square, square_ref.shape)
    if last:
        scale = lax.rsqrt(square / (piece * stages) + 1e-06)
        outs[1][...] = (cache * jnp.transpose(scale)[0:1, :]).astype(jnp.bfloat16)
    else:
        outs[1][...] = square
        outs[2][...] = cache


def finish(stage, stages, blocks, combine, here, own, gain, kv_matrix, rows, state):
    (total, width), (capacity, piece) = here.shape, blocks[0].shape
    heads = kv_matrix.shape[0]
    vmem = pl.BlockSpec(memory_space=pltpu.VMEM)
    hbm = pl.BlockSpec(memory_space=pl.ANY)
    shards = len(blocks)
    if stage == stages - 1:
        shapes = [((rows, width), jnp.bfloat16), ((heads, total), jnp.bfloat16)]
    else:
        shapes = [
            ((rows, piece), jnp.bfloat16),
            ((total, 128), jnp.float32),
            ((heads, total), jnp.float32),
        ]
    specs = [pl.BlockSpec(memory_space=pltpu.SMEM), hbm, hbm, vmem, hbm]
    specs += [hbm] * shards + [hbm] * min(len(state), 2) + [vmem] * max(len(state) - 2, 0)
    return pl.pallas_call(
        functools.partial(finish_body, stage, stages, shards),
        in_specs=specs,
        out_specs=[vmem] * len(shapes),
        out_shape=[jax.ShapeDtypeStruct(*shape) for shape in shapes],
        scratch_shapes=[
            pltpu.VMEM(combine.shape, jnp.bfloat16),
            pltpu.VMEM((total, piece), jnp.bfloat16),
            pltpu.VMEM((heads, piece), jnp.bfloat16),
            pltpu.VMEM((shards * capacity, piece), jnp.bfloat16),
            pltpu.VMEM((total, 128), jnp.float32),
            pltpu.VMEM((heads, total), jnp.float32),
            pltpu.SemaphoreType.DMA((shards + 5,)),
        ],
        compiler_params=pltpu.CompilerParams(vmem_limit_bytes=56 * 1024 * 1024),
        name="finish",
    )(own.reshape(1), combine, here, gain.reshape(1, width), kv_matrix, *blocks, *state)


def ffn_body(count, tile, pieces, *refs):
    inputs, weights = refs[:count], refs[count : count + 3]
    outputs = refs[count + 3 : count + 3 + sum(pieces)]
    rest = refs[count + 3 + sum(pieces) :]
    held, (rows_ref, acc_ref, sem) = rest[:3], rest[3:]
    size, width = inputs[0].shape
    steps = weights[0].shape[1] // tile
    loads = []
    for i in range(steps):
        span = slice(i * tile, (i + 1) * tile)
        places = [(slice(None), span), (slice(None), span), (span, slice(None))]
        loads.append(
            [
                pltpu.make_async_copy(
                    weights[k].at[place], held[k].at[place], sem.at[3 * i + k]
                )
                for k, place in enumerate(places)
            ]
        )
    ahead = min(2, steps)
    for copy in sum(loads[:ahead], []):
        copy.start()
    for i in range(count):
        rows_ref[i * size : (i + 1) * size, :] = inputs[i][...]
    for i in range(steps):
        span = slice(i * tile, (i + 1) * tile)
        for copy in loads[i]:
            copy.wait()
        for copy in loads[i + ahead] if i + ahead < steps else []:
            copy.start()
        rows = rows_ref[...]
        gate = jnp.dot(rows, held[0][:, span], preferred_element_type=jnp.float32)
        up = jnp.dot(rows, held[1][:, span], preferred_element_type=jnp.float32)
        hidden = (jax.nn.gelu(gate, approximate=True) * up).astype(jnp.bfloat16)
        part = jnp.dot(hidden, held[2][span, :], preferred_element_type=jnp.float32)
        if i > 0:
            part = acc_ref[...] + part
        if i < steps - 1:
            acc_ref[...] = part
    at = 0
    for i in range(count):
        piece = width // pieces[i]
        for j in range(pieces[i]):
            block = part[i * size : (i + 1) * size, j * piece : (j + 1) * piece]
            outputs[at][...] = block.astype(jnp.bfloat16)
            at += 1


def ffn(inputs, weights, pieces):
    count, (size, width) = len(inputs), inputs[0].shape
    hidden = weights[0].shape[1]
    tile = 256 if hidden % 256 == 0 else 128
    vmem = pl.BlockSpec(memory_space=pltpu.VMEM)
    shapes = [
        jax.ShapeDtypeStruct((size, width // parts), jnp.bfloat16)
        for parts in pieces
        for _ in range(parts)
    ]
    flat = pl.pallas_call(
        functools.partial(ffn_body, count, tile, pieces),
        in_specs=[vmem] * count + [pl.BlockSpec(memory_space=pl.ANY)] * 3,
        out_specs=[vmem] * len(shapes),
        out_shape=shapes,
        scratch_shapes=[
            pltpu.VMEM((width, hidden), jnp.bfloat16),
            pltpu.VMEM((width, hidden), jnp.bfloat16),
            pltpu.VMEM((hidden, width), jnp.bfloat16),
            pltpu.VMEM((count * size, width), jnp.bfloat16),
            pltpu.VMEM((count * size, width), jnp.float32),
            pltpu.SemaphoreType.DMA((3 * (hidden // tile),)),
        ],
        compiler_params=pltpu.CompilerParams(vmem_limit_bytes=56 * 1024 * 1024),
        cost_estimate=pl.CostEstimate(
            flops=6 * count * size * width * hidden,
            bytes_accessed=6 * width * hidden + 4 * count * size * width,
            transcendentals=count * size * hidden,
        ),
        name="ffn",
    )(*inputs, *weights)
    flat = list(flat)
    return [[flat.pop(0) for _ in range(parts)] for parts in pieces]


def local(
    tokens,
    norm_gain,
    router_weight,
    gate_weight,
    up_weight,
    down_weight,
    expert_picks,
    final_gain,
    kv_weight,
):
    shards = lax.axis_size("expert")
    groups = lax.axis_size("dp")
    own = lax.axis_index("expert")
    tok_rows, width = tokens.shape
    group_rows = shards * tok_rows
    order = jnp.arange(shards, dtype=jnp.int32) ^ own
    base = order * tok_rows
    picks = expert_picks[0][order]
    weights = (gate_weight[0], up_weight[0], down_weight[0])

    dense = fits([tokens] * shards)
    own_picks = lax.dynamic_slice_in_dim(expert_picks[0], own, 1, 0)
    far = {
        mask: (shuffle(tokens, "dp", mask), shuffle(own_picks, "dp", mask))
        for mask in range(groups - 1, 1, -1)
        if dense
    }
    blocks = plane_gather(tokens)
    inputs = {0: select(blocks, own_picks, base, norm_gain)}
    for mask in range(1, groups):
        if mask not in far:
            inputs[mask] = shuffle(inputs[0], "dp", mask)
    for mask, (spread, rows) in far.items():
        gathered = plane_gather(spread)
        inputs[mask] = select(gathered, rows, base, norm_gain)
    combine, here = prepare(
        blocks, picks, base, own, norm_gain, router_weight[:, order]
    )

    stages = 2 if dense else 1
    piece = width // stages
    split = lambda mask: stages if mask == 2 and dense else 1
    parts = {}
    sequence = [0] + list(range(groups - 1, 0, -1))
    half = max(groups // 2, 1)
    for start in range(0, groups, half):
        batch = sequence[start : start + half]
        result = ffn([inputs[m] for m in batch], weights, [split(m) for m in batch])
        parts.update(zip(batch, result))
    received = {
        mask: [shuffle(value, "dp", mask) for value in parts[mask]]
        for mask in range(1, groups)
    }
    received[0] = parts[0]
    kv_matrix = kv_weight.reshape(width, -1).T
    state = []
    for stage in range(stages):
        total = 0.0
        for mask in sequence:
            values = received[mask]
            if len(values) == stages:
                value = values[stage]
            else:
                value = values[0][:, stage * piece : (stage + 1) * piece]
            if stage > 0:
                value, _ = lax.optimization_barrier((value, summed))
            total += value.astype(jnp.float32)
        summed = total.astype(jnp.bfloat16)
        returned = plane_gather(summed)
        if not dense:
            moe_out, kv_rows = plain_finish(
                returned, combine, here, own, final_gain, kv_matrix, tok_rows
            )
            continue
        result = finish(
            stage, stages, returned, combine, here, own, final_gain, kv_matrix, tok_rows, state
        )
        if stage == stages - 1:
            moe_out, kv_rows = result
        else:
            state = [result[1], result[2]] + state[2:] + [result[0]]
    kv_cache = kv_rows.T.reshape((group_rows,) + kv_weight.shape[1:])
    return (moe_out, kv_cache)


def solution(mesh):
    in_specs = (
        P(("dp", "expert"), None),
        P(),
        P(),
        P("expert", None, "dp"),
        P("expert", None, "dp"),
        P("expert", "dp", None),
        P("dp", None, None),
        P(),
        P(None, "expert", None, None, None),
    )
    out_specs = (P(("dp", "expert"), None), P("dp", "expert", None, None, None))

    return jax.shard_map(local, mesh=mesh, in_specs=in_specs, out_specs=out_specs, check_vma=False)
```

profile of v0, /device:TPU:0, one launch (start us, length us, event | category | flops | bytes accessed | tf_op | source)
XLA Modules:
  0.0 170.8 jit_solution(13629278760319766829)
XLA Ops:
  1.2 2.6 %collective-permute-start.1 = (bf16[64,2048]{1,0:T(8,128)(2,1)}, bf16[64,2048]{1,0:T(8,128)(2,1)S(1)}, u32[]{:S(2)}, u32[]{:S(2)}) collective-permute-start(bf16[64,2048]{1,0:T(8,128)(2,1)} %refs_0_.3), channel_id=1, source_target_pairs={{0,2},{1,3},{2,0},{3,1},{4,6},{5,7},{6,4},{7,5},{8,10},{9,11},{10,... | collective-permute-start | bytes 786440 | tf_op jit(solution)/shard_map/ppermute | solution.py:13
  3.8 1.5 collective-permute-start.3
  5.3 3.6 %collective-permute-start.8 = (bf16[64,2048]{1,0:T(8,128)(2,1)}, bf16[64,2048]{1,0:T(8,128)(2,1)S(1)}, u32[]{:S(2)}, u32[]{:S(2)}) collective-permute-start(bf16[64,2048]{1,0:T(8,128)(2,1)} %refs_0_.3), channel_id=1, source_target_pairs={{0,24},{8,16},{16,8},{24,0},{1,25},{9,17},{17,9},{25,1},{2,26},{10... | collective-permute-start | bytes 786440 | tf_op jit(solution)/shard_map/ppermute | solution.py:13
  8.9 0.7 dynamic-slice_bitcast_fusion.picks_ref
  9.8 5.9 %collective-permute-done.7.picks_ref = s32[1,128]{1,0:T(1,128)S(1)} collective-permute-done((s32[1,128]{1,0:T(1,128)S(1)}, s32[1,128]{1,0:T(1,128)S(1)}, u32[]{:S(2)}, u32[]{:S(2)}) %collective-permute-start.7) | collective-permute-done | bytes 544 | tf_op jit(solution)/shard_map/ppermute | solution.py:13
  16.1 6.2 %collective-permute-start.18 = (bf16[64,2048]{1,0:T(8,128)(2,1)}, bf16[64,2048]{1,0:T(8,128)(2,1)S(1)}, u32[]{:S(2)}, u32[]{:S(2)}) collective-permute-start(bf16[64,2048]{1,0:T(8,128)(2,1)} %refs_0_.3), channel_id=1, source_target_pairs={{0,16},{8,24},{16,0},{24,8},{1,17},{9,25},{17,1},{25,9},{2,18},{10... | collective-permute-start | bytes 786440 | tf_op jit(solution)/shard_map/ppermute | solution.py:13
  22.9 1.5 collective-permute-start.10
  24.4 1.5 collective-permute-start.12
  25.9 7.4 %collective-permute-done.18.refs_0_ = bf16[64,2048]{1,0:T(8,128)(2,1)S(1)} collective-permute-done((bf16[64,2048]{1,0:T(8,128)(2,1)}, bf16[64,2048]{1,0:T(8,128)(2,1)S(1)}, u32[]{:S(2)}, u32[]{:S(2)}) %collective-permute-start.18) | collective-permute-done | bytes 262176 | tf_op jit(solution)/shard_map/ppermute | solution.py:13
  33.3 2.4 %collective-permute-start.14 = (bf16[64,2048]{1,0:T(8,128)(2,1)S(1)}, bf16[64,2048]{1,0:T(8,128)(2,1)S(1)}, u32[]{:S(2)}, u32[]{:S(2)}) collective-permute-start(bf16[64,2048]{1,0:T(8,128)(2,1)S(1)} %collective-permute-done.8.refs_0_), channel_id=1, source_target_pairs={{0,6},{1,7},{2,4},{3,5},{4,2},{5,3},{6,0},{7,1},{8,14},{9,15},{10,... | collective-permute-start | bytes 786440 | tf_op jit(solution)/shard_map/ppermute | solution.py:13
  36.8 4.5 %collective-permute-done.14.refs_6_ = bf16[64,2048]{1,0:T(8,128)(2,1)S(1)} collective-permute-done((bf16[64,2048]{1,0:T(8,128)(2,1)S(1)}, bf16[64,2048]{1,0:T(8,128)(2,1)S(1)}, u32[]{:S(2)}, u32[]{:S(2)}) %collective-permute-start.14) | collective-permute-done | bytes 262176 | tf_op jit(solution)/shard_map/ppermute | solution.py:13
  41.3 1.6 collective-permute-start.20
  42.9 1.5 collective-permute-start.22
  44.9 0.7 reshape.43.gain_ref
  45.6 0.9 copy-done.4
  46.5 1.2 select.3.refs_0_
  47.7 1.9 %collective-permute-start.26 = (bf16[128,2048]{1,0:T(8,128)(2,1)S(1)}, bf16[128,2048]{1,0:T(8,128)(2,1)S(1)}, u32[]{:S(2)}, u32[]{:S(2)}) collective-permute-start(bf16[128,2048]{1,0:T(8,128)(2,1)S(1)} %select.3.refs_0_), channel_id=1, source_target_pairs={{0,8},{8,0},{16,24},{24,16},{1,9},{9,1},{17,25},{25,17},{2,10},{10... | collective-permute-start | bytes 1572872 | tf_op jit(solution)/shard_map/ppermute | solution.py:13
  49.6 1.4 collective-permute-start.17
  51.0 1.2 select.4.refs_1_
  52.2 0.8 copy-done.2
  53.0 7.3 %collective-permute-done.17.picks_ref = s32[1,128]{1,0:T(1,128)S(1)} collective-permute-done((s32[1,128]{1,0:T(1,128)S(1)}, s32[1,128]{1,0:T(1,128)S(1)}, u32[]{:S(2)}, u32[]{:S(2)}) %collective-permute-start.17) | collective-permute-done | bytes 544 | tf_op jit(solution)/shard_map/ppermute | solution.py:13
  61.3 9.5 %ffn.2 = (bf16[128,2048]{1,0:T(8,128)(2,1)}, bf16[128,2048]{1,0:T(8,128)(2,1)}) custom-call(bf16[128,2048]{1,0:T(8,128)(2,1)} %copy-done.1, bf16[128,2048]{1,0:T(8,128)(2,1)} %copy-done.2, bf16[2048,1280]{1,0:T(8,128)(2,1)} %bitcast.16, bf16[2048,1280]{1,0:T(8,128)(2,1)} %bitcast.18, bf16[1280,2048]{1,0:T(8,128)(2,1)} %bitcast.20), custom_call_target="tpu_custom_call" | custom-call | flops 4026531840 | bytes 17825792 | tf_op jit(solution)/shard_map/ffn/pallas_call | solution.py:299
  70.9 2.8 %collective-permute-start.16 = (bf16[128,2048]{1,0:T(8,128)(2,1)}, bf16[128,2048]{1,0:T(8,128)(2,1)S(1)}, u32[]{:S(2)}, u32[]{:S(2)}) collective-permute-start(bf16[128,2048]{1,0:T(8,128)(2,1)} %get-tuple-element.21), channel_id=1, source_target_pairs={{0,24},{8,16},{16,8},{24,0},{1,25},{9,17},{17,9},{25,1},{2,26},{10... | collective-permute-start | bytes 1572872 | tf_op jit(solution)/shard_map/ppermute | solution.py:13
  73.8 1.2 select.5.refs_0_
  74.9 0.8 copy-done.3
  75.7 0.8 copy-done.16
  76.6 9.5 %ffn.3 = (bf16[128,1024]{1,0:T(8,128)(2,1)}, bf16[128,1024]{1,0:T(8,128)(2,1)}, bf16[128,2048]{1,0:T(8,128)(2,1)}) custom-call(bf16[128,2048]{1,0:T(8,128)(2,1)} %copy-done.3, bf16[128,2048]{1,0:T(8,128)(2,1)} %copy-done.16, bf16[2048,1280]{1,0:T(8,128)(2,1)} %bitcast.17, bf16[2048,1280]{1,0:T(8,128)(2,1)} %bitcast.19, bf16[1280,2048]{1,0:T(8,128)(2,1)} %bitcast.21), custom_call_target="tpu_custom_call" | custom-call | flops 4026531840 | bytes 17825792 | tf_op jit(solution)/shard_map/ffn/pallas_call | solution.py:299
  86.0 1.2 collective-permute-start.28
  87.3 1.4 collective-permute-start.27
  88.6 1.6 collective-permute-start.29
  90.3 13.4 %collective-permute-done.28 = bf16[128,2048]{1,0:T(8,128)(2,1)S(1)} collective-permute-done((bf16[128,2048]{1,0:T(8,128)(2,1)}, bf16[128,2048]{1,0:T(8,128)(2,1)S(1)}, u32[]{:S(2)}, u32[]{:S(2)}) %collective-permute-start.28) | collective-permute-done | bytes 524320 | tf_op jit(solution)/shard_map/ppermute | solution.py:13
  103.7 11.4 %collective-permute-done.27 = bf16[128,1024]{1,0:T(8,128)(2,1)S(1)} collective-permute-done((bf16[128,1024]{1,0:T(8,128)(2,1)}, bf16[128,1024]{1,0:T(8,128)(2,1)S(1)}, u32[]{:S(2)}, u32[]{:S(2)}) %collective-permute-start.27) | collective-permute-done | bytes 262176 | tf_op jit(solution)/shard_map/ppermute | solution.py:13
  115.3 5.4 %collective-permute-done.29 = bf16[128,1024]{1,0:T(8,128)(2,1)S(1)} collective-permute-done((bf16[128,1024]{1,0:T(8,128)(2,1)}, bf16[128,1024]{1,0:T(8,128)(2,1)S(1)}, u32[]{:S(2)}, u32[]{:S(2)}) %collective-permute-start.29) | collective-permute-done | bytes 262176 | tf_op jit(solution)/shard_map/ppermute | solution.py:13
  120.8 1.2 collective-permute-start.31
  122.1 0.8 collective-permute-start.33
  122.9 1.2 collective-permute-start.38
  124.1 1.1 collective-permute-start.40
  125.1 1.3 collective-permute-start.42
  126.4 3.8 %collective-permute-done.31.refs_7_ = bf16[128,1024]{1,0:T(8,128)(2,1)S(1)} collective-permute-done((bf16[128,1024]{1,0:T(8,128)(2,1)S(1)}, bf16[128,1024]{1,0:T(8,128)(2,1)S(1)}, u32[]{:S(2)}, u32[]{:S(2)}) %collective-permute-start.31) | collective-permute-done | bytes 262176 | tf_op jit(solution)/shard_map/ppermute | solution.py:13
  130.2 1.3 collective-permute-start.35
  131.5 4.3 %collective-permute-done.38.refs_7_ = bf16[128,1024]{1,0:T(8,128)(2,1)S(1)} collective-permute-done((bf16[128,1024]{1,0:T(8,128)(2,1)S(1)}, bf16[128,1024]{1,0:T(8,128)(2,1)S(1)}, u32[]{:S(2)}, u32[]{:S(2)}) %collective-permute-start.38) | collective-permute-done | bytes 262176 | tf_op jit(solution)/shard_map/ppermute | solution.py:13
  135.9 11.0 %collective-permute-done.40.refs_9_ = bf16[128,1024]{1,0:T(8,128)(2,1)S(1)} collective-permute-done((bf16[128,1024]{1,0:T(8,128)(2,1)S(1)}, bf16[128,1024]{1,0:T(8,128)(2,1)S(1)}, u32[]{:S(2)}, u32[]{:S(2)}) %collective-permute-start.40) | collective-permute-done | bytes 262176 | tf_op jit(solution)/shard_map/ppermute | solution.py:13
  148.6 1.1 gather_fusion
  150.3 1.0 copy.11
  151.9 4.7 %prepare.1 = (bf16[512,1024]{1,0:T(8,128)(2,1)}, bf16[512,2048]{1,0:T(8,128)(2,1)}) custom-call(s32[8]{0:T(128)} %copy-done.13, s32[1]{0:T(128)} %bitcast.own_ref.refs_0_, s32[8,128]{1,0:T(8,128)} %gather_fusion, bf16[1,2048]{1,0:T(2,128)(2,1)} %copy-done.12, bf16[2048,8]{1,0:T(8,128)(2,1)} %bitcast.24, bf16[64,2048]{1,0:T(8,128)(2,1)} %refs_0_.3, ...), custom_call_target="tpu_custom_call" | custom-call | tf_op jit(solution)/shard_map/prepare/pallas_call | solution.py:136
  156.7 6.6 %finish.2 = (bf16[64,1024]{1,0:T(8,128)(2,1)}, f32[512,128]{1,0:T(8,128)}, f32[768,512]{1,0:T(8,128)}) custom-call(s32[1]{0:T(128)} %bitcast.own_ref.refs_0_, bf16[512,1024]{1,0:T(8,128)(2,1)} %get-tuple-element.18.refs_1_, bf16[512,2048]{1,0:T(8,128)(2,1)} %get-tuple-element.19.refs_2_, bf16[1,2048]{1,0:T(2,128)(2,1)} %reshape.44.refs_3_, ...), custom_call_target="tpu_custom_call" | custom-call | tf_op jit(solution)/shard_map/finish/pallas_call | solution.py:222
  163.4 0.6 copy-done.25
  164.1 6.5 %finish.3 = (bf16[64,2048]{1,0:T(8,128)(2,1)}, bf16[768,512]{1,0:T(8,128)(2,1)}) custom-call(s32[1]{0:T(128)} %bitcast.own_ref.refs_0_, bf16[512,1024]{1,0:T(8,128)(2,1)} %get-tuple-element.18.refs_1_, bf16[512,2048]{1,0:T(8,128)(2,1)} %get-tuple-element.19.refs_2_, bf16[1,2048]{1,0:T(2,128)(2,1)} %reshape.44.refs_3_, bf16[768,2048]{1,0:T(8,128)(2,1)} %bitcast.23, ...), custom_call_target="tpu_custom_call" | custom-call | tf_op jit(solution)/shard_map/finish/pallas_call | solution.py:222
  (124 shorter events, 7.8 us)
Async XLA Ops:
  0.6 149.1 %copy-start = (bf16[2048,8]{0,1:T(8,128)(2,1)S(1)}, bf16[2048,8]{0,1:T(8,128)(2,1)}, u32[]{:S(2)}) copy-start(bf16[2048,8]{0,1:T(8,128)(2,1)} %param.11) | copy-start | bytes 98308
  0.6 15.5 %collective-permute-start = (bf16[64,2048]{1,0:T(8,128)(2,1)}, bf16[64,2048]{1,0:T(8,128)(2,1)S(1)}, u32[]{:S(2)}, u32[]{:S(2)}) collective-permute-start(bf16[64,2048]{1,0:T(8,128)(2,1)} %refs_0_.3), channel_id=1, source_target_pairs={{0,1},{1,0},{2,3},{3,2},{4,5},{5,4},{6,7},{7,6},{8,9},{9,8},{10,11... | collective-permute-start | bytes 786440 | tf_op jit(solution)/shard_map/ppermute | solution.py:13
  1.2 21.2 %collective-permute-start.1 = (bf16[64,2048]{1,0:T(8,128)(2,1)}, bf16[64,2048]{1,0:T(8,128)(2,1)S(1)}, u32[]{:S(2)}, u32[]{:S(2)}) collective-permute-start(bf16[64,2048]{1,0:T(8,128)(2,1)} %refs_0_.3), channel_id=1, source_target_pairs={{0,2},{1,3},{2,0},{3,1},{4,6},{5,7},{6,4},{7,5},{8,10},{9,11},{10,... | collective-permute-start | bytes 786440 | tf_op jit(solution)/shard_map/ppermute | solution.py:13
  3.8 18.6 %collective-permute-start.3 = (bf16[64,2048]{1,0:T(8,128)(2,1)}, bf16[64,2048]{1,0:T(8,128)(2,1)S(1)}, u32[]{:S(2)}, u32[]{:S(2)}) collective-permute-start(bf16[64,2048]{1,0:T(8,128)(2,1)} %refs_0_.3), channel_id=1, source_target_pairs={{0,4},{1,5},{2,6},{3,7},{4,0},{5,1},{6,2},{7,3},{8,12},{9,13},{10,... | collective-permute-start | bytes 786440 | tf_op jit(solution)/shard_map/ppermute | solution.py:13
  5.3 17.6 %collective-permute-start.8 = (bf16[64,2048]{1,0:T(8,128)(2,1)}, bf16[64,2048]{1,0:T(8,128)(2,1)S(1)}, u32[]{:S(2)}, u32[]{:S(2)}) collective-permute-start(bf16[64,2048]{1,0:T(8,128)(2,1)} %refs_0_.3), channel_id=1, source_target_pairs={{0,24},{8,16},{16,8},{24,0},{1,25},{9,17},{17,9},{25,1},{2,26},{10... | collective-permute-start | bytes 786440 | tf_op jit(solution)/shard_map/ppermute | solution.py:13
  9.6 6.1 %collective-permute-start.7 = (s32[1,128]{1,0:T(1,128)S(1)}, s32[1,128]{1,0:T(1,128)S(1)}, u32[]{:S(2)}, u32[]{:S(2)}) collective-permute-start(s32[1,128]{1,0:T(1,128)S(1)} %dynamic-slice_bitcast_fusion.picks_ref), channel_id=1, source_target_pairs={{0,24},{8,16},{16,8},{24,0},{1,25},{9,17},{17,9},{25,1},{2,26},{10... | collective-permute-start | bytes 1544 | tf_op jit(solution)/shard_map/ppermute | solution.py:13
  15.7 8.7 %collective-permute-start.5 = (bf16[64,2048]{1,0:T(8,128)(2,1)}, bf16[64,2048]{1,0:T(8,128)(2,1)S(1)}, u32[]{:S(2)}, u32[]{:S(2)}) collective-permute-start(bf16[64,2048]{1,0:T(8,128)(2,1)} %refs_0_.3), channel_id=1, source_target_pairs={{0,6},{1,7},{2,4},{3,5},{4,2},{5,3},{6,0},{7,1},{8,14},{9,15},{10,... | collective-permute-start | bytes 786440 | tf_op jit(solution)/shard_map/ppermute | solution.py:13
  16.1 54.7 %copy-start.5 = (bf16[64,2048]{1,0:T(8,128)(2,1)}, bf16[64,2048]{1,0:T(8,128)(2,1)S(1)}, u32[]{:S(2)}) copy-start(bf16[64,2048]{1,0:T(8,128)(2,1)S(1)} %collective-permute-done.refs_1_) | copy-start | bytes 786436
  16.1 17.2 %collective-permute-start.18 = (bf16[64,2048]{1,0:T(8,128)(2,1)}, bf16[64,2048]{1,0:T(8,128)(2,1)S(1)}, u32[]{:S(2)}, u32[]{:S(2)}) collective-permute-start(bf16[64,2048]{1,0:T(8,128)(2,1)} %refs_0_.3), channel_id=1, source_target_pairs={{0,16},{8,24},{16,0},{24,8},{1,17},{9,25},{17,1},{25,9},{2,18},{10... | collective-permute-start | bytes 786440 | tf_op jit(solution)/shard_map/ppermute | solution.py:13
  22.4 13.4 %collective-permute-start.2 = (bf16[64,2048]{1,0:T(8,128)(2,1)S(1)}, bf16[64,2048]{1,0:T(8,128)(2,1)S(1)}, u32[]{:S(2)}, u32[]{:S(2)}) collective-permute-start(bf16[64,2048]{1,0:T(8,128)(2,1)S(1)} %collective-permute-done.1.refs_2_), channel_id=1, source_target_pairs={{0,1},{1,0},{2,3},{3,2},{4,5},{5,4},{6,7},{7,6},{8,9},{9,8},{10,11... | collective-permute-start | bytes 786440 | tf_op jit(solution)/shard_map/ppermute | solution.py:13
  22.4 13.4 %collective-permute-start.4 = (bf16[64,2048]{1,0:T(8,128)(2,1)S(1)}, bf16[64,2048]{1,0:T(8,128)(2,1)S(1)}, u32[]{:S(2)}, u32[]{:S(2)}) collective-permute-start(bf16[64,2048]{1,0:T(8,128)(2,1)S(1)} %collective-permute-done.3.refs_4_), channel_id=1, source_target_pairs={{0,1},{1,0},{2,3},{3,2},{4,5},{5,4},{6,7},{7,6},{8,9},{9,8},{10,11... | collective-permute-start | bytes 786440 | tf_op jit(solution)/shard_map/ppermute | solution.py:13
  22.9 13.4 %collective-permute-start.10 = (bf16[64,2048]{1,0:T(8,128)(2,1)S(1)}, bf16[64,2048]{1,0:T(8,128)(2,1)S(1)}, u32[]{:S(2)}, u32[]{:S(2)}) collective-permute-start(bf16[64,2048]{1,0:T(8,128)(2,1)S(1)} %collective-permute-done.8.refs_0_), channel_id=1, source_target_pairs={{0,2},{1,3},{2,0},{3,1},{4,6},{5,7},{6,4},{7,5},{8,10},{9,11},{10,... | collective-permute-start | bytes 786440 | tf_op jit(solution)/shard_map/ppermute | solution.py:13
  24.4 12.0 %collective-permute-start.12 = (bf16[64,2048]{1,0:T(8,128)(2,1)S(1)}, bf16[64,2048]{1,0:T(8,128)(2,1)S(1)}, u32[]{:S(2)}, u32[]{:S(2)}) collective-permute-start(bf16[64,2048]{1,0:T(8,128)(2,1)S(1)} %collective-permute-done.8.refs_0_), channel_id=1, source_target_pairs={{0,4},{1,5},{2,6},{3,7},{4,0},{5,1},{6,2},{7,3},{8,12},{9,13},{10,... | collective-permute-start | bytes 786440 | tf_op jit(solution)/shard_map/ppermute | solution.py:13
  33.3 8.0 %collective-permute-start.14 = (bf16[64,2048]{1,0:T(8,128)(2,1)S(1)}, bf16[64,2048]{1,0:T(8,128)(2,1)S(1)}, u32[]{:S(2)}, u32[]{:S(2)}) collective-permute-start(bf16[64,2048]{1,0:T(8,128)(2,1)S(1)} %collective-permute-done.8.refs_0_), channel_id=1, source_target_pairs={{0,6},{1,7},{2,4},{3,5},{4,2},{5,3},{6,0},{7,1},{8,14},{9,15},{10,... | collective-permute-start | bytes 786440 | tf_op jit(solution)/shard_map/ppermute | solution.py:13
  35.8 5.5 %collective-permute-start.6 = (bf16[64,2048]{1,0:T(8,128)(2,1)S(1)}, bf16[64,2048]{1,0:T(8,128)(2,1)S(1)}, u32[]{:S(2)}, u32[]{:S(2)}) collective-permute-start(bf16[64,2048]{1,0:T(8,128)(2,1)S(1)} %collective-permute-done.5.refs_6_), channel_id=1, source_target_pairs={{0,1},{1,0},{2,3},{3,2},{4,5},{5,4},{6,7},{7,6},{8,9},{9,8},{10,11... | collective-permute-start | bytes 786440 | tf_op jit(solution)/shard_map/ppermute | solution.py:13
  35.8 7.1 %collective-permute-start.9 = (bf16[64,2048]{1,0:T(8,128)(2,1)S(1)}, bf16[64,2048]{1,0:T(8,128)(2,1)S(1)}, u32[]{:S(2)}, u32[]{:S(2)}) collective-permute-start(bf16[64,2048]{1,0:T(8,128)(2,1)S(1)} %collective-permute-done.8.refs_0_), channel_id=1, source_target_pairs={{0,1},{1,0},{2,3},{3,2},{4,5},{5,4},{6,7},{7,6},{8,9},{9,8},{10,11... | collective-permute-start | bytes 786440 | tf_op jit(solution)/shard_map/ppermute | solution.py:13
  36.3 8.1 %collective-permute-start.11 = (bf16[64,2048]{1,0:T(8,128)(2,1)S(1)}, bf16[64,2048]{1,0:T(8,128)(2,1)S(1)}, u32[]{:S(2)}, u32[]{:S(2)}) collective-permute-start(bf16[64,2048]{1,0:T(8,128)(2,1)S(1)} %collective-permute-done.10.refs_2_), channel_id=1, source_target_pairs={{0,1},{1,0},{2,3},{3,2},{4,5},{5,4},{6,7},{7,6},{8,9},{9,8},{10,11... | collective-permute-start | bytes 786440 | tf_op jit(solution)/shard_map/ppermute | solution.py:13
  36.4 11.3 %collective-permute-start.13 = (bf16[64,2048]{1,0:T(8,128)(2,1)S(1)}, bf16[64,2048]{1,0:T(8,128)(2,1)S(1)}, u32[]{:S(2)}, u32[]{:S(2)}) collective-permute-start(bf16[64,2048]{1,0:T(8,128)(2,1)S(1)} %collective-permute-done.12.refs_4_), channel_id=1, source_target_pairs={{0,1},{1,0},{2,3},{3,2},{4,5},{5,4},{6,7},{7,6},{8,9},{9,8},{10,11... | collective-permute-start | bytes 786440 | tf_op jit(solution)/shard_map/ppermute | solution.py:13
  41.3 8.3 %collective-permute-start.15 = (bf16[64,2048]{1,0:T(8,128)(2,1)S(1)}, bf16[64,2048]{1,0:T(8,128)(2,1)S(1)}, u32[]{:S(2)}, u32[]{:S(2)}) collective-permute-start(bf16[64,2048]{1,0:T(8,128)(2,1)S(1)} %collective-permute-done.14.refs_6_), channel_id=1, source_target_pairs={{0,1},{1,0},{2,3},{3,2},{4,5},{5,4},{6,7},{7,6},{8,9},{9,8},{10,11... | collective-permute-start | bytes 786440 | tf_op jit(solution)/shard_map/ppermute | solution.py:13
  41.3 18.9 %collective-permute-start.20 = (bf16[64,2048]{1,0:T(8,128)(2,1)S(1)}, bf16[64,2048]{1,0:T(8,128)(2,1)S(1)}, u32[]{:S(2)}, u32[]{:S(2)}) collective-permute-start(bf16[64,2048]{1,0:T(8,128)(2,1)S(1)} %collective-permute-done.18.refs_0_), channel_id=1, source_target_pairs={{0,2},{1,3},{2,0},{3,1},{4,6},{5,7},{6,4},{7,5},{8,10},{9,11},{10,... | collective-permute-start | bytes 786440 | tf_op jit(solution)/shard_map/ppermute | solution.py:13
  42.9 17.9 %collective-permute-start.22 = (bf16[64,2048]{1,0:T(8,128)(2,1)S(1)}, bf16[64,2048]{1,0:T(8,128)(2,1)S(1)}, u32[]{:S(2)}, u32[]{:S(2)}) collective-permute-start(bf16[64,2048]{1,0:T(8,128)(2,1)S(1)} %collective-permute-done.18.refs_0_), channel_id=1, source_target_pairs={{0,4},{1,5},{2,6},{3,7},{4,0},{5,1},{6,2},{7,3},{8,12},{9,13},{10,... | collective-permute-start | bytes 786440 | tf_op jit(solution)/shard_map/ppermute | solution.py:13
  44.4 16.5 %collective-permute-start.24 = (bf16[64,2048]{1,0:T(8,128)(2,1)S(1)}, bf16[64,2048]{1,0:T(8,128)(2,1)S(1)}, u32[]{:S(2)}, u32[]{:S(2)}) collective-permute-start(bf16[64,2048]{1,0:T(8,128)(2,1)S(1)} %collective-permute-done.18.refs_0_), channel_id=1, source_target_pairs={{0,6},{1,7},{2,4},{3,5},{4,2},{5,3},{6,0},{7,1},{8,14},{9,15},{10,... | collective-permute-start | bytes 786440 | tf_op jit(solution)/shard_map/ppermute | solution.py:13
  47.7 28.0 %collective-permute-start.26 = (bf16[128,2048]{1,0:T(8,128)(2,1)S(1)}, bf16[128,2048]{1,0:T(8,128)(2,1)S(1)}, u32[]{:S(2)}, u32[]{:S(2)}) collective-permute-start(bf16[128,2048]{1,0:T(8,128)(2,1)S(1)} %select.3.refs_0_), channel_id=1, source_target_pairs={{0,8},{8,0},{16,24},{24,16},{1,9},{9,1},{17,25},{25,17},{2,10},{10... | collective-permute-start | bytes 1572872 | tf_op jit(solution)/shard_map/ppermute | solution.py:13
  49.6 10.6 %collective-permute-start.17 = (s32[1,128]{1,0:T(1,128)S(1)}, s32[1,128]{1,0:T(1,128)S(1)}, u32[]{:S(2)}, u32[]{:S(2)}) collective-permute-start(s32[1,128]{1,0:T(1,128)S(1)} %dynamic-slice_bitcast_fusion.picks_ref), channel_id=1, source_target_pairs={{0,16},{8,24},{16,0},{24,8},{1,17},{9,25},{17,1},{25,9},{2,18},{10... | collective-permute-start | bytes 1544 | tf_op jit(solution)/shard_map/ppermute | solution.py:13
  60.3 10.7 %collective-permute-start.19 = (bf16[64,2048]{1,0:T(8,128)(2,1)S(1)}, bf16[64,2048]{1,0:T(8,128)(2,1)S(1)}, u32[]{:S(2)}, u32[]{:S(2)}) collective-permute-start(bf16[64,2048]{1,0:T(8,128)(2,1)S(1)} %collective-permute-done.18.refs_0_), channel_id=1, source_target_pairs={{0,1},{1,0},{2,3},{3,2},{4,5},{5,4},{6,7},{7,6},{8,9},{9,8},{10,11... | collective-permute-start | bytes 786440 | tf_op jit(solution)/shard_map/ppermute | solution.py:13
  60.3 13.5 %collective-permute-start.21 = (bf16[64,2048]{1,0:T(8,128)(2,1)S(1)}, bf16[64,2048]{1,0:T(8,128)(2,1)S(1)}, u32[]{:S(2)}, u32[]{:S(2)}) collective-permute-start(bf16[64,2048]{1,0:T(8,128)(2,1)S(1)} %collective-permute-done.20.refs_2_), channel_id=1, source_target_pairs={{0,1},{1,0},{2,3},{3,2},{4,5},{5,4},{6,7},{7,6},{8,9},{9,8},{10,11... | collective-permute-start | bytes 786440 | tf_op jit(solution)/shard_map/ppermute | solution.py:13
  60.8 13.0 %collective-permute-start.23 = (bf16[64,2048]{1,0:T(8,128)(2,1)S(1)}, bf16[64,2048]{1,0:T(8,128)(2,1)S(1)}, u32[]{:S(2)}, u32[]{:S(2)}) collective-permute-start(bf16[64,2048]{1,0:T(8,128)(2,1)S(1)} %collective-permute-done.22.refs_4_), channel_id=1, source_target_pairs={{0,1},{1,0},{2,3},{3,2},{4,5},{5,4},{6,7},{7,6},{8,9},{9,8},{10,11... | collective-permute-start | bytes 786440 | tf_op jit(solution)/shard_map/ppermute | solution.py:13
  60.8 12.9 %collective-permute-start.25 = (bf16[64,2048]{1,0:T(8,128)(2,1)S(1)}, bf16[64,2048]{1,0:T(8,128)(2,1)S(1)}, u32[]{:S(2)}, u32[]{:S(2)}) collective-permute-start(bf16[64,2048]{1,0:T(8,128)(2,1)S(1)} %collective-permute-done.24.refs_6_), channel_id=1, source_target_pairs={{0,1},{1,0},{2,3},{3,2},{4,5},{5,4},{6,7},{7,6},{8,9},{9,8},{10,11... | collective-permute-start | bytes 786440 | tf_op jit(solution)/shard_map/ppermute | solution.py:13
  70.9 19.3 %collective-permute-start.16 = (bf16[128,2048]{1,0:T(8,128)(2,1)}, bf16[128,2048]{1,0:T(8,128)(2,1)S(1)}, u32[]{:S(2)}, u32[]{:S(2)}) collective-permute-start(bf16[128,2048]{1,0:T(8,128)(2,1)} %get-tuple-element.21), channel_id=1, source_target_pairs={{0,24},{8,16},{16,8},{24,0},{1,25},{9,17},{17,9},{25,1},{2,26},{10... | collective-permute-start | bytes 1572872 | tf_op jit(solution)/shard_map/ppermute | solution.py:13
  75.7 72.8 %copy-start.29 = (s32[1,8,128]{2,1,0:T(8,128)S(1)}, s32[1,8,128]{2,1,0:T(8,128)}, u32[]{:S(2)}) copy-start(s32[1,8,128]{2,1,0:T(8,128)} %param.15) | copy-start | bytes 12292
  86.0 65.3 %copy-start.30 = (bf16[2048]{0:T(1024)(128)(2,1)S(1)}, bf16[2048]{0:T(1024)(128)(2,1)}, u32[]{:S(2)}) copy-start(bf16[2048]{0:T(1024)(128)(2,1)} %param.16) | copy-start | bytes 12292
  86.0 17.7 %collective-permute-start.28 = (bf16[128,2048]{1,0:T(8,128)(2,1)}, bf16[128,2048]{1,0:T(8,128)(2,1)S(1)}, u32[]{:S(2)}, u32[]{:S(2)}) collective-permute-start(bf16[128,2048]{1,0:T(8,128)(2,1)} %get-tuple-element.23), channel_id=1, source_target_pairs={{0,8},{8,0},{16,24},{24,16},{1,9},{9,1},{17,25},{25,17},{2,10},{10... | collective-permute-start | bytes 1572872 | tf_op jit(solution)/shard_map/ppermute | solution.py:13
  87.3 27.8 %collective-permute-start.27 = (bf16[128,1024]{1,0:T(8,128)(2,1)}, bf16[128,1024]{1,0:T(8,128)(2,1)S(1)}, u32[]{:S(2)}, u32[]{:S(2)}) collective-permute-start(bf16[128,1024]{1,0:T(8,128)(2,1)} %get-tuple-element.22), channel_id=1, source_target_pairs={{0,16},{8,24},{16,0},{24,8},{1,17},{9,25},{17,1},{25,9},{2,18},{10... | collective-permute-start | bytes 786440 | tf_op jit(solution)/shard_map/ppermute | solution.py:13
  88.6 32.0 %collective-permute-start.29 = (bf16[128,1024]{1,0:T(8,128)(2,1)}, bf16[128,1024]{1,0:T(8,128)(2,1)S(1)}, u32[]{:S(2)}, u32[]{:S(2)}) collective-permute-start(bf16[128,1024]{1,0:T(8,128)(2,1)} %get-tuple-element.26), channel_id=1, source_target_pairs={{0,16},{8,24},{16,0},{24,8},{1,17},{9,25},{17,1},{25,9},{2,18},{10... | collective-permute-start | bytes 786440 | tf_op jit(solution)/shard_map/ppermute | solution.py:13
  120.8 9.4 %collective-permute-start.31 = (bf16[128,1024]{1,0:T(8,128)(2,1)S(1)}, bf16[128,1024]{1,0:T(8,128)(2,1)S(1)}, u32[]{:S(2)}, u32[]{:S(2)}) collective-permute-start(bf16[128,1024]{1,0:T(8,128)(2,1)S(1)} %add_convert_fusion.refs_5_), channel_id=1, source_target_pairs={{0,2},{1,3},{2,0},{3,1},{4,6},{5,7},{6,4},{7,5},{8,10},{9,11},{10,... | collective-permute-start | bytes 786440 | tf_op jit(solution)/shard_map/ppermute | solution.py:13
  122.1 9.5 %collective-permute-start.33 = (bf16[128,1024]{1,0:T(8,128)(2,1)S(1)}, bf16[128,1024]{1,0:T(8,128)(2,1)S(1)}, u32[]{:S(2)}, u32[]{:S(2)}) collective-permute-start(bf16[128,1024]{1,0:T(8,128)(2,1)S(1)} %add_convert_fusion.refs_5_), channel_id=1, source_target_pairs={{0,4},{1,5},{2,6},{3,7},{4,0},{5,1},{6,2},{7,3},{8,12},{9,13},{10,... | collective-permute-start | bytes 786440 | tf_op jit(solution)/shard_map/ppermute | solution.py:13
  122.9 12.9 %collective-permute-start.38 = (bf16[128,1024]{1,0:T(8,128)(2,1)S(1)}, bf16[128,1024]{1,0:T(8,128)(2,1)S(1)}, u32[]{:S(2)}, u32[]{:S(2)}) collective-permute-start(bf16[128,1024]{1,0:T(8,128)(2,1)S(1)} %add_convert_fusion.1.refs_5_), channel_id=1, source_target_pairs={{0,2},{1,3},{2,0},{3,1},{4,6},{5,7},{6,4},{7,5},{8,10},{9,11},{10,... | collective-permute-start | bytes 786440 | tf_op jit(solution)/shard_map/ppermute | solution.py:13
  124.1 22.8 %collective-permute-start.40 = (bf16[128,1024]{1,0:T(8,128)(2,1)S(1)}, bf16[128,1024]{1,0:T(8,128)(2,1)S(1)}, u32[]{:S(2)}, u32[]{:S(2)}) collective-permute-start(bf16[128,1024]{1,0:T(8,128)(2,1)S(1)} %add_convert_fusion.1.refs_5_), channel_id=1, source_target_pairs={{0,4},{1,5},{2,6},{3,7},{4,0},{5,1},{6,2},{7,3},{8,12},{9,13},{10,... | collective-permute-start | bytes 786440 | tf_op jit(solution)/shard_map/ppermute | solution.py:13
  125.1 21.8 %collective-permute-start.42 = (bf16[128,1024]{1,0:T(8,128)(2,1)S(1)}, bf16[128,1024]{1,0:T(8,128)(2,1)S(1)}, u32[]{:S(2)}, u32[]{:S(2)}) collective-permute-start(bf16[128,1024]{1,0:T(8,128)(2,1)S(1)} %add_convert_fusion.1.refs_5_), channel_id=1, source_target_pairs={{0,6},{1,7},{2,4},{3,5},{4,2},{5,3},{6,0},{7,1},{8,14},{9,15},{10,... | collective-permute-start | bytes 786440 | tf_op jit(solution)/shard_map/ppermute | solution.py:13
  130.2 17.2 %collective-permute-start.35 = (bf16[128,1024]{1,0:T(8,128)(2,1)S(1)}, bf16[128,1024]{1,0:T(8,128)(2,1)S(1)}, u32[]{:S(2)}, u32[]{:S(2)}) collective-permute-start(bf16[128,1024]{1,0:T(8,128)(2,1)S(1)} %add_convert_fusion.refs_5_), channel_id=1, source_target_pairs={{0,6},{1,7},{2,4},{3,5},{4,2},{5,3},{6,0},{7,1},{8,14},{9,15},{10,... | collective-permute-start | bytes 786440 | tf_op jit(solution)/shard_map/ppermute | solution.py:13
  131.5 16.0 %collective-permute-start.37 = (bf16[128,1024]{1,0:T(8,128)(2,1)S(1)}, bf16[128,1024]{1,0:T(8,128)(2,1)S(1)}, u32[]{:S(2)}, u32[]{:S(2)}) collective-permute-start(bf16[128,1024]{1,0:T(8,128)(2,1)S(1)} %add_convert_fusion.1.refs_5_), channel_id=1, source_target_pairs={{0,1},{1,0},{2,3},{3,2},{4,5},{5,4},{6,7},{7,6},{8,9},{9,8},{10,11... | collective-permute-start | bytes 786440 | tf_op jit(solution)/shard_map/ppermute | solution.py:13
  135.9 12.1 %collective-permute-start.39 = (bf16[128,1024]{1,0:T(8,128)(2,1)S(1)}, bf16[128,1024]{1,0:T(8,128)(2,1)S(1)}, u32[]{:S(2)}, u32[]{:S(2)}) collective-permute-start(bf16[128,1024]{1,0:T(8,128)(2,1)S(1)} %collective-permute-done.38.refs_7_), channel_id=1, source_target_pairs={{0,1},{1,0},{2,3},{3,2},{4,5},{5,4},{6,7},{7,6},{8,9},{9,8},{10,11... | collective-permute-start | bytes 786440 | tf_op jit(solution)/shard_map/ppermute | solution.py:13
  146.9 1.5 collective-permute-start.41
  146.9 9.7 %collective-permute-start.43 = (bf16[128,1024]{1,0:T(8,128)(2,1)S(1)}, bf16[128,1024]{1,0:T(8,128)(2,1)}, u32[]{:S(2)}, u32[]{:S(2)}) collective-permute-start(bf16[128,1024]{1,0:T(8,128)(2,1)S(1)} %collective-permute-done.42.refs_11_), channel_id=1, source_target_pairs={{0,1},{1,0},{2,3},{3,2},{4,5},{5,4},{6,7},{7,6},{8,9},{9,8},{10,11... | collective-permute-start | bytes 786440 | tf_op jit(solution)/shard_map/ppermute | solution.py:13
  147.4 15.9 %collective-permute-start.30 = (bf16[128,1024]{1,0:T(8,128)(2,1)S(1)}, bf16[128,1024]{1,0:T(8,128)(2,1)S(1)}, u32[]{:S(2)}, u32[]{:S(2)}) collective-permute-start(bf16[128,1024]{1,0:T(8,128)(2,1)S(1)} %add_convert_fusion.refs_5_), channel_id=1, source_target_pairs={{0,1},{1,0},{2,3},{3,2},{4,5},{5,4},{6,7},{7,6},{8,9},{9,8},{10,11... | collective-permute-start | bytes 786440 | tf_op jit(solution)/shard_map/ppermute | solution.py:13
  147.5 15.8 %collective-permute-start.32 = (bf16[128,1024]{1,0:T(8,128)(2,1)S(1)}, bf16[128,1024]{1,0:T(8,128)(2,1)S(1)}, u32[]{:S(2)}, u32[]{:S(2)}) collective-permute-start(bf16[128,1024]{1,0:T(8,128)(2,1)S(1)} %collective-permute-done.31.refs_7_), channel_id=1, source_target_pairs={{0,1},{1,0},{2,3},{3,2},{4,5},{5,4},{6,7},{7,6},{8,9},{9,8},{10,11... | collective-permute-start | bytes 786440 | tf_op jit(solution)/shard_map/ppermute | solution.py:13
  147.9 15.4 %collective-permute-start.34 = (bf16[128,1024]{1,0:T(8,128)(2,1)S(1)}, bf16[128,1024]{1,0:T(8,128)(2,1)}, u32[]{:S(2)}, u32[]{:S(2)}) collective-permute-start(bf16[128,1024]{1,0:T(8,128)(2,1)S(1)} %collective-permute-done.33.refs_9_), channel_id=1, source_target_pairs={{0,1},{1,0},{2,3},{3,2},{4,5},{5,4},{6,7},{7,6},{8,9},{9,8},{10,11... | collective-permute-start | bytes 786440 | tf_op jit(solution)/shard_map/ppermute | solution.py:13
  148.4 14.9 %collective-permute-start.36 = (bf16[128,1024]{1,0:T(8,128)(2,1)S(1)}, bf16[128,1024]{1,0:T(8,128)(2,1)}, u32[]{:S(2)}, u32[]{:S(2)}) collective-permute-start(bf16[128,1024]{1,0:T(8,128)(2,1)S(1)} %collective-permute-done.35.refs_11_), channel_id=1, source_target_pairs={{0,1},{1,0},{2,3},{3,2},{4,5},{5,4},{6,7},{7,6},{8,9},{9,8},{10,11... | collective-permute-start | bytes 786440 | tf_op jit(solution)/shard_map/ppermute | solution.py:13
  (27 other events, 562.6 us)
where the time goes:
time: 171 us
  waiting for transfers between devices  74.9 us (44%)
  starting transfers between devices  45 us (26%)
  Pallas kernels  40.3 us (24%)
  local copies, waits for them, and re-layouts  8.96 us (5%)
    ppermute x44, waiting for transfers between devices, shuffle(): return lax.ppermute(value, axis, [(i, i ^ mask) for i in range(size)])  74.9 us
    ppermute x44, starting transfers between devices, shuffle(): return lax.ppermute(value, axis, [(i, i ^ mask) for i in range(size)])  45 us
    pallas_call x2, Pallas kernels, ffn(): pl.pallas_call(functools.partial(ffn_body, count, tile, pieces), in_specs...  19 us
    pallas_call x2, Pallas kernels, finish(): pl.pallas_call(functools.partial(finish_body, stage, stages, shards), in_...  13.1 us
    pallas_call x1, Pallas kernels, prepare(): pl.pallas_call(prepare_body, in_specs=[smem, smem] + [vmem] * (3 + shards...  4.71 us
    unnamed x62, local copies, waits for them, and re-layouts  4.2 us
    pallas_call x3, Pallas kernels, select(): pl.pallas_call(select_body, in_specs=[pl.BlockSpec(memory_space=pltpu.SME...  3.52 us
  transfers between devices with their start and end apart: 44, of which 11 were waited for; matrix products, arithmetic and copies ran while one was open for 3% of the time, Pallas kernels for 20%

commit v1 on v0

--- a/solution.py
+++ b/solution.py
@@ -8,9 +8,9 @@
 from jax.sharding import PartitionSpec as P
 
 
-def shuffle(value, axis, mask):
+def shuffle(value, axis, mask, keep=lambda i: True):
     size = lax.axis_size(axis)
-    return lax.ppermute(value, axis, [(i, i ^ mask) for i in range(size)])
+    return lax.ppermute(value, axis, [(i, i ^ mask) for i in range(size) if keep(i)])
 
 
 def plane_gather(value):
@@ -99,7 +99,7 @@
         in_specs=[pl.BlockSpec(memory_space=pltpu.SMEM)] + [vmem] * (2 + len(blocks)),
         out_specs=vmem,
         out_shape=jax.ShapeDtypeStruct((capacity, width), jnp.bfloat16),
-        compiler_params=pltpu.CompilerParams(vmem_limit_bytes=48 * 1024 * 1024),
+        compiler_params=pltpu.CompilerParams(vmem_limit_bytes=12 * 1024 * 1024),
         name="select",
     )(base, picks.reshape(1, capacity), gain.reshape(1, width), *blocks)
 
@@ -141,7 +141,7 @@
             jax.ShapeDtypeStruct((shards * rows, shards * capacity), jnp.bfloat16),
             jax.ShapeDtypeStruct((shards * rows, width), jnp.bfloat16),
         ],
-        compiler_params=pltpu.CompilerParams(vmem_limit_bytes=56 * 1024 * 1024),
+        compiler_params=pltpu.CompilerParams(vmem_limit_bytes=24 * 1024 * 1024),
         name="prepare",
     )(base, own.reshape(1), picks, gain.reshape(1, width), router, *blocks)
 
@@ -233,7 +233,7 @@
             pltpu.VMEM((heads, total), jnp.float32),
             pltpu.SemaphoreType.DMA((shards + 5,)),
         ],
-        compiler_params=pltpu.CompilerParams(vmem_limit_bytes=56 * 1024 * 1024),
+        compiler_params=pltpu.CompilerParams(vmem_limit_bytes=28 * 1024 * 1024),
         name="finish",
     )(own.reshape(1), combine, here, gain.reshape(1, width), kv_matrix, *blocks, *state)
 
@@ -298,7 +298,7 @@
     ]
     flat = pl.pallas_call(
         functools.partial(ffn_body, count, tile, pieces),
-        in_specs=[vmem] * count + [pl.BlockSpec(memory_space=pl.ANY)] * 3,
+        in_specs=[vmem] * count + [pl.BlockSpec(memory_space=pltpu.HBM)] * 3,
         out_specs=[vmem] * len(shapes),
         out_shape=shapes,
         scratch_shapes=[
@@ -309,7 +309,7 @@
             pltpu.VMEM((count * size, width), jnp.float32),
             pltpu.SemaphoreType.DMA((3 * (hidden // tile),)),
         ],
-        compiler_params=pltpu.CompilerParams(vmem_limit_bytes=56 * 1024 * 1024),
+        compiler_params=pltpu.CompilerParams(vmem_limit_bytes=50 * 1024 * 1024),
         cost_estimate=pl.CostEstimate(
             flops=6 * count * size * width * hidden,
             bytes_accessed=6 * width * hidden + 4 * count * size * width,
@@ -363,7 +363,7 @@
 
     stages = 2 if dense else 1
     piece = width // stages
-    split = lambda mask: stages if mask == 2 and dense else 1
+    split = lambda mask: stages if mask in (1, 2) and dense else 1
     parts = {}
     sequence = [0] + list(range(groups - 1, 0, -1))
     half = max(groups // 2, 1)
@@ -371,8 +371,26 @@
         batch = sequence[start : start + half]
         result = ffn([inputs[m] for m in batch], weights, [split(m) for m in batch])
         parts.update(zip(batch, result))
+    last = groups - 1
+    close = lambda i: groups <= 2 or abs(i - (i ^ last)) == 1
+    if groups > 2:
+        passed = [
+            shuffle(value, "dp", 1, lambda i: not close(i))
+            for value in parts[last]
+        ]
+        passed = jnp.concatenate(passed, axis=1) if len(passed) > 1 else passed[0]
+        size = passed.shape[1] // len(parts[last - 1])
+        parts[last - 1] = [
+            (value.astype(jnp.float32) + passed[:, j * size : (j + 1) * size]).astype(
+                jnp.bfloat16
+            )
+            for j, value in enumerate(parts[last - 1])
+        ]
     received = {
-        mask: [shuffle(value, "dp", mask) for value in parts[mask]]
+        mask: [
+            shuffle(value, "dp", mask, close if mask == last else lambda i: True)
+            for value in parts[mask]
+        ]
         for mask in range(1, groups)
     }
     received[0] = parts[0]
@@ -382,12 +400,11 @@
         total = 0.0
         for mask in sequence:
             values = received[mask]
-            if len(values) == stages:
-                value = values[stage]
-            else:
-                value = values[0][:, stage * piece : (stage + 1) * piece]
+            value = values[stage] if len(values) == stages else values[0]
             if stage > 0:
                 value, _ = lax.optimization_barrier((value, summed))
+            if value.shape[1] != piece:
+                value = value[:, stage * piece : (stage + 1) * piece]
             total += value.astype(jnp.float32)
         summed = total.astype(jnp.bfloat16)
         returned = plane_gather(summed)

time: 171 us -> 163 us (0.953)
  waiting for transfers between devices: 74.9 us -> 44.3 us
  starting transfers between devices: 45 us -> 64.4 us
  local copies, waits for them, and re-layouts: 8.96 us -> 22.1 us
  Pallas kernels: 40.3 us -> 29.4 us
    ppermute x44 -> x46, waiting for transfers between devices: 74.9 us -> 44.3 us  [shuffle(): lax.ppermute(value, axis, [(i, i ^ mask) for i in range(size) if keep(i)])]
    ppermute x44 -> x46, starting transfers between devices: 45 us -> 64.4 us  [shuffle(): lax.ppermute(value, axis, [(i, i ^ mask) for i in range(size) if keep(i)])]
    unnamed x62 -> x66, local copies, waits for them, and re-layouts: 4.2 us -> 18.6 us
    pallas_call x2, Pallas kernels: 13.1 us -> 8.8 us  [finish(): pl.pallas_call(functools.partial(finish_body, stage, stages, shards), in_...]
    pallas_call x2, Pallas kernels: 19 us -> 14.8 us  [ffn(): pl.pallas_call(functools.partial(ffn_body, count, tile, pieces), in_specs...]
    pallas_call x1, Pallas kernels: 4.71 us -> 2.26 us  [prepare(): pl.pallas_call(prepare_body, in_specs=[smem, smem] + [vmem] * (3 + shards...]
  transfers between devices with their start and end apart: 44 -> 46, of which waited for: 11 -> 11; matrix products, arithmetic and copies ran while one was open for 3% -> 3% of each run, Pallas kernels for 20% -> 15%
where the time goes in v1:
time: 163 us
  starting transfers between devices  64.4 us (40%)
  waiting for transfers between devices  44.3 us (27%)
  Pallas kernels  29.4 us (18%)
  local copies, waits for them, and re-layouts  22.1 us (14%)
    ppermute x46, starting transfers between devices, shuffle(): lax.ppermute(value, axis, [(i, i ^ mask) for i in range(size) if keep(i)])  64.4 us
    ppermute x46, waiting for transfers between devices, shuffle(): lax.ppermute(value, axis, [(i, i ^ mask) for i in range(size) if keep(i)])  44.3 us
    unnamed x66, local copies, waits for them, and re-layouts  18.6 us
    pallas_call x2, Pallas kernels, ffn(): pl.pallas_call(functools.partial(ffn_body, count, tile, pieces), in_specs...  14.8 us
    pallas_call x2, Pallas kernels, finish(): pl.pallas_call(functools.partial(finish_body, stage, stages, shards), in_...  8.8 us
    pallas_call x3, Pallas kernels, select(): pl.pallas_call(select_body, in_specs=[pl.BlockSpec(memory_space=pltpu.SME...  3.52 us
  transfers between devices with their start and end apart: 46, of which 11 were waited for; matrix products, arithmetic and copies ran while one was open for 3% of the time, Pallas kernels for 15%

profile of v1, /device:TPU:0, one launch (start us, length us, event | category | flops | bytes accessed | tf_op | source)
XLA Modules:
  0.0 162.7 jit_solution(10781670950988251453)
XLA Ops:
  0.6 4.1 %collective-permute-start.18 = (bf16[64,2048]{1,0:T(8,128)(2,1)}, bf16[64,2048]{1,0:T(8,128)(2,1)S(1)}, u32[]{:S(2)}, u32[]{:S(2)}) collective-permute-start(bf16[64,2048]{1,0:T(8,128)(2,1)} %refs_0_.3), channel_id=1, source_target_pairs={{0,16},{8,24},{16,0},{24,8},{1,17},{9,25},{17,1},{25,9},{2,18},{10... | collective-permute-start | bytes 786440 | tf_op jit(solution)/shard_map/ppermute | solution.py:13
  4.8 1.5 collective-permute-start.1
  6.3 1.5 collective-permute-start.3
  7.8 1.3 collective-permute-start.8
  9.8 2.5 %collective-permute-start.7 = (s32[1,128]{1,0:T(1,128)S(1)}, s32[1,128]{1,0:T(1,128)S(1)}, u32[]{:S(2)}, u32[]{:S(2)}) collective-permute-start(s32[1,128]{1,0:T(1,128)S(1)} %dynamic-slice_bitcast_fusion.picks_ref), channel_id=1, source_target_pairs={{0,24},{8,16},{16,8},{24,0},{1,25},{9,17},{17,9},{25,1},{2,26},{10... | collective-permute-start | bytes 1544 | tf_op jit(solution)/shard_map/ppermute | solution.py:13
  12.3 5.9 %collective-permute-done.7.picks_ref = s32[1,128]{1,0:T(1,128)S(1)} collective-permute-done((s32[1,128]{1,0:T(1,128)S(1)}, s32[1,128]{1,0:T(1,128)S(1)}, u32[]{:S(2)}, u32[]{:S(2)}) %collective-permute-start.7) | collective-permute-done | bytes 544 | tf_op jit(solution)/shard_map/ppermute | solution.py:13
  18.2 2.4 %collective-permute-start.5 = (bf16[64,2048]{1,0:T(8,128)(2,1)}, bf16[64,2048]{1,0:T(8,128)(2,1)S(1)}, u32[]{:S(2)}, u32[]{:S(2)}) collective-permute-start(bf16[64,2048]{1,0:T(8,128)(2,1)} %refs_0_.3), channel_id=1, source_target_pairs={{0,6},{1,7},{2,4},{3,5},{4,2},{5,3},{6,0},{7,1},{8,14},{9,15},{10,... | collective-permute-start | bytes 786440 | tf_op jit(solution)/shard_map/ppermute | solution.py:13
  20.6 2.8 %collective-permute-done.18.refs_0_ = bf16[64,2048]{1,0:T(8,128)(2,1)S(1)} collective-permute-done((bf16[64,2048]{1,0:T(8,128)(2,1)}, bf16[64,2048]{1,0:T(8,128)(2,1)S(1)}, u32[]{:S(2)}, u32[]{:S(2)}) %collective-permute-start.18) | collective-permute-done | bytes 262176 | tf_op jit(solution)/shard_map/ppermute | solution.py:13
  24.0 1.8 %collective-permute-start.10 = (bf16[64,2048]{1,0:T(8,128)(2,1)S(1)}, bf16[64,2048]{1,0:T(8,128)(2,1)S(1)}, u32[]{:S(2)}, u32[]{:S(2)}) collective-permute-start(bf16[64,2048]{1,0:T(8,128)(2,1)S(1)} %collective-permute-done.8.refs_0_), channel_id=1, source_target_pairs={{0,2},{1,3},{2,0},{3,1},{4,6},{5,7},{6,4},{7,5},{8,10},{9,11},{10,... | collective-permute-start | bytes 786440 | tf_op jit(solution)/shard_map/ppermute | solution.py:13
  26.4 1.4 collective-permute-start.12
  27.9 1.4 collective-permute-start.14
  29.9 3.3 %collective-permute-done.10.refs_2_ = bf16[64,2048]{1,0:T(8,128)(2,1)S(1)} collective-permute-done((bf16[64,2048]{1,0:T(8,128)(2,1)S(1)}, bf16[64,2048]{1,0:T(8,128)(2,1)S(1)}, u32[]{:S(2)}, u32[]{:S(2)}) %collective-permute-start.10) | collective-permute-done | bytes 262176 | tf_op jit(solution)/shard_map/ppermute | solution.py:13
  33.2 6.6 %collective-permute-done.12.refs_4_ = bf16[64,2048]{1,0:T(8,128)(2,1)S(1)} collective-permute-done((bf16[64,2048]{1,0:T(8,128)(2,1)S(1)}, bf16[64,2048]{1,0:T(8,128)(2,1)S(1)}, u32[]{:S(2)}, u32[]{:S(2)}) %collective-permute-start.12) | collective-permute-done | bytes 262176 | tf_op jit(solution)/shard_map/ppermute | solution.py:13
  41.1 1.3 collective-permute-start.22
  42.4 1.4 collective-permute-start.24
  43.8 13.4 %collective-permute-start.17 = (s32[1,128]{1,0:T(1,128)S(1)}, s32[1,128]{1,0:T(1,128)S(1)}, u32[]{:S(2)}, u32[]{:S(2)}) collective-permute-start(s32[1,128]{1,0:T(1,128)S(1)} %dynamic-slice_bitcast_fusion.picks_ref), channel_id=1, source_target_pairs={{0,16},{8,24},{16,0},{24,8},{1,17},{9,25},{17,1},{25,9},{2,18},{10... | collective-permute-start | bytes 1544 | tf_op jit(solution)/shard_map/ppermute | solution.py:13
  57.9 0.9 copy-done.3
  58.8 1.2 select.3.refs_0_
  60.2 1.2 select.4.refs_1_
  62.5 7.4 %ffn.2 = (bf16[128,2048]{1,0:T(8,128)(2,1)S(1)}, bf16[128,2048]{1,0:T(8,128)(2,1)S(1)}) custom-call(bf16[128,2048]{1,0:T(8,128)(2,1)S(1)} %select.3.refs_0_, bf16[128,2048]{1,0:T(8,128)(2,1)S(1)} %select.4.refs_1_, bf16[2048,1280]{1,0:T(8,128)(2,1)} %bitcast.19, bf16[2048,1280]{1,0:T(8,128)(2,1)} %bitcast.21, bf16[1280,2048]{1,0:T(8,128)(2,1)} %bitcast.23), custom_call_target="tpu_custom_call" | custom-call | flops 4026531840 | bytes 17825792 | tf_op jit(solution)/shard_map/ffn/pallas_call | solution.py:299
  69.9 6.9 %collective-permute-start.27 = (bf16[128,2048]{1,0:T(8,128)(2,1)S(1)}, bf16[128,2048]{1,0:T(8,128)(2,1)S(1)}, u32[]{:S(2)}, u32[]{:S(2)}) collective-permute-start(bf16[128,2048]{1,0:T(8,128)(2,1)S(1)} %get-tuple-element.22), channel_id=1, source_target_pairs={{0,8},{24,16},{1,9},{25,17},{2,10},{26,18},{3,11},{27,19},{4,12},{... | collective-permute-start | bytes 1572872 | tf_op jit(solution)/shard_map/ppermute | solution.py:13
  77.7 1.2 select.5.refs_0_
  78.9 7.4 %ffn.3 = (bf16[128,1024]{1,0:T(8,128)(2,1)S(1)}, bf16[128,1024]{1,0:T(8,128)(2,1)S(1)}, bf16[128,1024]{1,0:T(8,128)(2,1)S(1)}, bf16[128,1024]{1,0:T(8,128)(2,1)S(1)}) custom-call(bf16[128,2048]{1,0:T(8,128)(2,1)S(1)} %select.5.refs_0_, bf16[128,2048]{1,0:T(8,128)(2,1)S(1)} %collective-permute-done.26.refs_1_, bf16[2048,1280]{1,0:T(8,128)(2,1)} %bitcast.20, ...), custom_call_target="tpu_custom_call" | custom-call | flops 4026531840 | bytes 17825792 | tf_op jit(solution)/shard_map/ffn/pallas_call | solution.py:299
  86.4 3.0 %collective-permute-start.29 = (bf16[128,1024]{1,0:T(8,128)(2,1)S(1)}, bf16[128,1024]{1,0:T(8,128)(2,1)S(1)}, u32[]{:S(2)}, u32[]{:S(2)}) collective-permute-start(bf16[128,1024]{1,0:T(8,128)(2,1)S(1)} %get-tuple-element.24), channel_id=1, source_target_pairs={{0,8},{8,0},{16,24},{24,16},{1,9},{9,1},{17,25},{25,17},{2,10},{10... | collective-permute-start | bytes 786440 | tf_op jit(solution)/shard_map/ppermute | solution.py:13
  89.6 4.1 %collective-permute-start.28 = (bf16[128,1024]{1,0:T(8,128)(2,1)S(1)}, bf16[128,1024]{1,0:T(8,128)(2,1)S(1)}, u32[]{:S(2)}, u32[]{:S(2)}) collective-permute-start(bf16[128,1024]{1,0:T(8,128)(2,1)S(1)} %get-tuple-element.37), channel_id=1, source_target_pairs={{0,16},{8,24},{16,0},{24,8},{1,17},{9,25},{17,1},{25,9},{2,18},{10... | collective-permute-start | bytes 786440 | tf_op jit(solution)/shard_map/ppermute | solution.py:13
  93.8 7.6 %collective-permute-done.29 = bf16[128,1024]{1,0:T(8,128)(2,1)S(1)} collective-permute-done((bf16[128,1024]{1,0:T(8,128)(2,1)S(1)}, bf16[128,1024]{1,0:T(8,128)(2,1)S(1)}, u32[]{:S(2)}, u32[]{:S(2)}) %collective-permute-start.29) | collective-permute-done | bytes 262176 | tf_op jit(solution)/shard_map/ppermute | solution.py:13
  101.4 10.7 %collective-permute-done.28 = bf16[128,1024]{1,0:T(8,128)(2,1)S(1)} collective-permute-done((bf16[128,1024]{1,0:T(8,128)(2,1)S(1)}, bf16[128,1024]{1,0:T(8,128)(2,1)S(1)}, u32[]{:S(2)}, u32[]{:S(2)}) %collective-permute-start.28) | collective-permute-done | bytes 262176 | tf_op jit(solution)/shard_map/ppermute | solution.py:13
  113.0 1.3 collective-permute-start.42
  114.4 1.4 collective-permute-start.44
  117.4 1.2 collective-permute-start.33
  118.7 1.5 collective-permute-start.35
  121.1 4.4 %collective-permute-start.37 = (bf16[128,1024]{1,0:T(8,128)(2,1)}, bf16[128,1024]{1,0:T(8,128)(2,1)}, u32[]{:S(2)}, u32[]{:S(2)}) collective-permute-start(bf16[128,1024]{1,0:T(8,128)(2,1)} %add_convert_fusion.refs_5_), channel_id=1, source_target_pairs={{0,6},{1,7},{2,4},{3,5},{4,2},{5,3},{6,0},{7,1},{8,14},{9,15},{10,... | collective-permute-start | bytes 786440 | tf_op jit(solution)/shard_map/ppermute | solution.py:13
  128.1 4.3 %collective-permute-done.35.refs_9_ = bf16[128,1024]{1,0:T(8,128)(2,1)} collective-permute-done((bf16[128,1024]{1,0:T(8,128)(2,1)}, bf16[128,1024]{1,0:T(8,128)(2,1)}, u32[]{:S(2)}, u32[]{:S(2)}) %collective-permute-start.35) | collective-permute-done | bytes 262176 | tf_op jit(solution)/shard_map/ppermute | solution.py:13
  132.5 1.3 collective-permute-done.37.refs_11_
  136.4 1.0 copy.11
  138.0 1.0 copy-done.2
  139.0 0.9 copy-done.6
  140.0 0.9 copy-done.8
  140.9 0.9 copy-done.10
  141.9 0.9 copy-done.12
  143.8 0.9 copy-done.16
  144.7 0.9 copy-done.18
  145.7 2.3 %prepare.1 = (bf16[512,1024]{1,0:T(8,128)(2,1)S(1)}, bf16[512,2048]{1,0:T(8,128)(2,1)S(1)}) custom-call(s32[8]{0:T(128)S(1)} %xor_multiply_fusion.base_ref, s32[1]{0:T(128)} %bitcast.own_ref.refs_0_, s32[8,128]{1,0:T(8,128)S(1)} %gather_fusion, bf16[1,2048]{1,0:T(2,128)(2,1)S(1)} %reshape.43.gain_ref, bf16[2048,8]{1,0:T(8,128)(2,1)S(1)} %bitcast.18, ...), custom_call_target="tpu_custom_call" | custom-call | tf_op jit(solution)/shard_map/prepare/pallas_call | solution.py:136
  149.8 0.9 copy-done.24
  150.8 0.9 copy-done.26
  152.7 0.9 copy-done.30
  153.6 3.8 %finish.2 = (bf16[64,1024]{1,0:T(8,128)(2,1)S(1)}, f32[512,128]{1,0:T(8,128)S(1)}, f32[768,512]{1,0:T(8,128)S(1)}) custom-call(s32[1]{0:T(128)} %bitcast.own_ref.refs_0_, bf16[512,1024]{1,0:T(8,128)(2,1)S(1)} %get-tuple-element.19.refs_1_, bf16[512,2048]{1,0:T(8,128)(2,1)S(1)} %get-tuple-element.20.refs_2_, bf16[1,2048]{1,0:T(2,128)(2,1)S(1)} %reshape.44.refs_3_, ...), custom_call_target="tpu_custom_call" | custom-call | tf_op jit(solution)/shard_map/finish/pallas_call | solution.py:222
  157.5 5.0 %finish.3 = (bf16[64,2048]{1,0:T(8,128)(2,1)}, bf16[768,512]{1,0:T(8,128)(2,1)}) custom-call(s32[1]{0:T(128)} %bitcast.own_ref.refs_0_, bf16[512,1024]{1,0:T(8,128)(2,1)S(1)} %get-tuple-element.19.refs_1_, bf16[512,2048]{1,0:T(8,128)(2,1)S(1)} %get-tuple-element.20.refs_2_, bf16[1,2048]{1,0:T(2,128)(2,1)S(1)} %reshape.44.refs_3_, ...), custom_call_target="tpu_custom_call" | custom-call | tf_op jit(solution)/shard_map/finish/pallas_call | solution.py:222
  (130 shorter events, 20.0 us)
Async XLA Ops:
  0.6 135.1 %copy-start = (bf16[2048,8]{0,1:T(8,128)(2,1)S(1)}, bf16[2048,8]{0,1:T(8,128)(2,1)}, u32[]{:S(2)}) copy-start(bf16[2048,8]{0,1:T(8,128)(2,1)} %param.11) | copy-start | bytes 98308
  0.6 22.7 %collective-permute-start.18 = (bf16[64,2048]{1,0:T(8,128)(2,1)}, bf16[64,2048]{1,0:T(8,128)(2,1)S(1)}, u32[]{:S(2)}, u32[]{:S(2)}) collective-permute-start(bf16[64,2048]{1,0:T(8,128)(2,1)} %refs_0_.3), channel_id=1, source_target_pairs={{0,16},{8,24},{16,0},{24,8},{1,17},{9,25},{17,1},{25,9},{2,18},{10... | collective-permute-start | bytes 786440 | tf_op jit(solution)/shard_map/ppermute | solution.py:13
  4.8 18.6 %collective-permute-start.1 = (bf16[64,2048]{1,0:T(8,128)(2,1)}, bf16[64,2048]{1,0:T(8,128)(2,1)S(1)}, u32[]{:S(2)}, u32[]{:S(2)}) collective-permute-start(bf16[64,2048]{1,0:T(8,128)(2,1)} %refs_0_.3), channel_id=1, source_target_pairs={{0,2},{1,3},{2,0},{3,1},{4,6},{5,7},{6,4},{7,5},{8,10},{9,11},{10,... | collective-permute-start | bytes 786440 | tf_op jit(solution)/shard_map/ppermute | solution.py:13
  6.3 17.6 %collective-permute-start.3 = (bf16[64,2048]{1,0:T(8,128)(2,1)}, bf16[64,2048]{1,0:T(8,128)(2,1)S(1)}, u32[]{:S(2)}, u32[]{:S(2)}) collective-permute-start(bf16[64,2048]{1,0:T(8,128)(2,1)} %refs_0_.3), channel_id=1, source_target_pairs={{0,4},{1,5},{2,6},{3,7},{4,0},{5,1},{6,2},{7,3},{8,12},{9,13},{10,... | collective-permute-start | bytes 786440 | tf_op jit(solution)/shard_map/ppermute | solution.py:13
  7.8 16.2 %collective-permute-start.8 = (bf16[64,2048]{1,0:T(8,128)(2,1)}, bf16[64,2048]{1,0:T(8,128)(2,1)S(1)}, u32[]{:S(2)}, u32[]{:S(2)}) collective-permute-start(bf16[64,2048]{1,0:T(8,128)(2,1)} %refs_0_.3), channel_id=1, source_target_pairs={{0,24},{8,16},{16,8},{24,0},{1,25},{9,17},{17,9},{25,1},{2,26},{10... | collective-permute-start | bytes 786440 | tf_op jit(solution)/shard_map/ppermute | solution.py:13
  9.8 8.3 %collective-permute-start.7 = (s32[1,128]{1,0:T(1,128)S(1)}, s32[1,128]{1,0:T(1,128)S(1)}, u32[]{:S(2)}, u32[]{:S(2)}) collective-permute-start(s32[1,128]{1,0:T(1,128)S(1)} %dynamic-slice_bitcast_fusion.picks_ref), channel_id=1, source_target_pairs={{0,24},{8,16},{16,8},{24,0},{1,25},{9,17},{17,9},{25,1},{2,26},{10... | collective-permute-start | bytes 1544 | tf_op jit(solution)/shard_map/ppermute | solution.py:13
  18.2 8.3 %collective-permute-start.5 = (bf16[64,2048]{1,0:T(8,128)(2,1)}, bf16[64,2048]{1,0:T(8,128)(2,1)S(1)}, u32[]{:S(2)}, u32[]{:S(2)}) collective-permute-start(bf16[64,2048]{1,0:T(8,128)(2,1)} %refs_0_.3), channel_id=1, source_target_pairs={{0,6},{1,7},{2,4},{3,5},{4,2},{5,3},{6,0},{7,1},{8,14},{9,15},{10,... | collective-permute-start | bytes 786440 | tf_op jit(solution)/shard_map/ppermute | solution.py:13
  23.4 4.5 %collective-permute-start = (bf16[64,2048]{1,0:T(8,128)(2,1)}, bf16[64,2048]{1,0:T(8,128)(2,1)S(1)}, u32[]{:S(2)}, u32[]{:S(2)}) collective-permute-start(bf16[64,2048]{1,0:T(8,128)(2,1)} %refs_0_.3), channel_id=1, source_target_pairs={{0,1},{1,0},{2,3},{3,2},{4,5},{5,4},{6,7},{7,6},{8,9},{9,8},{10,11... | collective-permute-start | bytes 786440 | tf_op jit(solution)/shard_map/ppermute | solution.py:13
  23.4 5.9 %collective-permute-start.2 = (bf16[64,2048]{1,0:T(8,128)(2,1)S(1)}, bf16[64,2048]{1,0:T(8,128)(2,1)S(1)}, u32[]{:S(2)}, u32[]{:S(2)}) collective-permute-start(bf16[64,2048]{1,0:T(8,128)(2,1)S(1)} %collective-permute-done.1.refs_2_), channel_id=1, source_target_pairs={{0,1},{1,0},{2,3},{3,2},{4,5},{5,4},{6,7},{7,6},{8,9},{9,8},{10,11... | collective-permute-start | bytes 786440 | tf_op jit(solution)/shard_map/ppermute | solution.py:13
  23.9 5.4 %collective-permute-start.4 = (bf16[64,2048]{1,0:T(8,128)(2,1)S(1)}, bf16[64,2048]{1,0:T(8,128)(2,1)S(1)}, u32[]{:S(2)}, u32[]{:S(2)}) collective-permute-start(bf16[64,2048]{1,0:T(8,128)(2,1)S(1)} %collective-permute-done.3.refs_4_), channel_id=1, source_target_pairs={{0,1},{1,0},{2,3},{3,2},{4,5},{5,4},{6,7},{7,6},{8,9},{9,8},{10,11... | collective-permute-start | bytes 786440 | tf_op jit(solution)/shard_map/ppermute | solution.py:13
  24.0 9.2 %collective-permute-start.10 = (bf16[64,2048]{1,0:T(8,128)(2,1)S(1)}, bf16[64,2048]{1,0:T(8,128)(2,1)S(1)}, u32[]{:S(2)}, u32[]{:S(2)}) collective-permute-start(bf16[64,2048]{1,0:T(8,128)(2,1)S(1)} %collective-permute-done.8.refs_0_), channel_id=1, source_target_pairs={{0,2},{1,3},{2,0},{3,1},{4,6},{5,7},{6,4},{7,5},{8,10},{9,11},{10,... | collective-permute-start | bytes 786440 | tf_op jit(solution)/shard_map/ppermute | solution.py:13
  26.4 13.3 %collective-permute-start.12 = (bf16[64,2048]{1,0:T(8,128)(2,1)S(1)}, bf16[64,2048]{1,0:T(8,128)(2,1)S(1)}, u32[]{:S(2)}, u32[]{:S(2)}) collective-permute-start(bf16[64,2048]{1,0:T(8,128)(2,1)S(1)} %collective-permute-done.8.refs_0_), channel_id=1, source_target_pairs={{0,4},{1,5},{2,6},{3,7},{4,0},{5,1},{6,2},{7,3},{8,12},{9,13},{10,... | collective-permute-start | bytes 786440 | tf_op jit(solution)/shard_map/ppermute | solution.py:13
  27.9 11.9 %collective-permute-start.14 = (bf16[64,2048]{1,0:T(8,128)(2,1)S(1)}, bf16[64,2048]{1,0:T(8,128)(2,1)S(1)}, u32[]{:S(2)}, u32[]{:S(2)}) collective-permute-start(bf16[64,2048]{1,0:T(8,128)(2,1)S(1)} %collective-permute-done.8.refs_0_), channel_id=1, source_target_pairs={{0,6},{1,7},{2,4},{3,5},{4,2},{5,3},{6,0},{7,1},{8,14},{9,15},{10,... | collective-permute-start | bytes 786440 | tf_op jit(solution)/shard_map/ppermute | solution.py:13
  29.3 11.0 %collective-permute-start.6 = (bf16[64,2048]{1,0:T(8,128)(2,1)S(1)}, bf16[64,2048]{1,0:T(8,128)(2,1)S(1)}, u32[]{:S(2)}, u32[]{:S(2)}) collective-permute-start(bf16[64,2048]{1,0:T(8,128)(2,1)S(1)} %collective-permute-done.5.refs_6_), channel_id=1, source_target_pairs={{0,1},{1,0},{2,3},{3,2},{4,5},{5,4},{6,7},{7,6},{8,9},{9,8},{10,11... | collective-permute-start | bytes 786440 | tf_op jit(solution)/shard_map/ppermute | solution.py:13
  29.4 11.7 %collective-permute-start.9 = (bf16[64,2048]{1,0:T(8,128)(2,1)S(1)}, bf16[64,2048]{1,0:T(8,128)(2,1)S(1)}, u32[]{:S(2)}, u32[]{:S(2)}) collective-permute-start(bf16[64,2048]{1,0:T(8,128)(2,1)S(1)} %collective-permute-done.8.refs_0_), channel_id=1, source_target_pairs={{0,1},{1,0},{2,3},{3,2},{4,5},{5,4},{6,7},{7,6},{8,9},{9,8},{10,11... | collective-permute-start | bytes 786440 | tf_op jit(solution)/shard_map/ppermute | solution.py:13
  33.2 9.2 %collective-permute-start.11 = (bf16[64,2048]{1,0:T(8,128)(2,1)S(1)}, bf16[64,2048]{1,0:T(8,128)(2,1)S(1)}, u32[]{:S(2)}, u32[]{:S(2)}) collective-permute-start(bf16[64,2048]{1,0:T(8,128)(2,1)S(1)} %collective-permute-done.10.refs_2_), channel_id=1, source_target_pairs={{0,1},{1,0},{2,3},{3,2},{4,5},{5,4},{6,7},{7,6},{8,9},{9,8},{10,11... | collective-permute-start | bytes 786440 | tf_op jit(solution)/shard_map/ppermute | solution.py:13
  39.8 4.0 %collective-permute-start.13 = (bf16[64,2048]{1,0:T(8,128)(2,1)S(1)}, bf16[64,2048]{1,0:T(8,128)(2,1)S(1)}, u32[]{:S(2)}, u32[]{:S(2)}) collective-permute-start(bf16[64,2048]{1,0:T(8,128)(2,1)S(1)} %collective-permute-done.12.refs_4_), channel_id=1, source_target_pairs={{0,1},{1,0},{2,3},{3,2},{4,5},{5,4},{6,7},{7,6},{8,9},{9,8},{10,11... | collective-permute-start | bytes 786440 | tf_op jit(solution)/shard_map/ppermute | solution.py:13
  39.8 20.2 %collective-permute-start.15 = (bf16[64,2048]{1,0:T(8,128)(2,1)S(1)}, bf16[64,2048]{1,0:T(8,128)(2,1)S(1)}, u32[]{:S(2)}, u32[]{:S(2)}) collective-permute-start(bf16[64,2048]{1,0:T(8,128)(2,1)S(1)} %collective-permute-done.14.refs_6_), channel_id=1, source_target_pairs={{0,1},{1,0},{2,3},{3,2},{4,5},{5,4},{6,7},{7,6},{8,9},{9,8},{10,11... | collective-permute-start | bytes 786440 | tf_op jit(solution)/shard_map/ppermute | solution.py:13
  40.3 21.1 %collective-permute-start.20 = (bf16[64,2048]{1,0:T(8,128)(2,1)S(1)}, bf16[64,2048]{1,0:T(8,128)(2,1)S(1)}, u32[]{:S(2)}, u32[]{:S(2)}) collective-permute-start(bf16[64,2048]{1,0:T(8,128)(2,1)S(1)} %collective-permute-done.18.refs_0_), channel_id=1, source_target_pairs={{0,2},{1,3},{2,0},{3,1},{4,6},{5,7},{6,4},{7,5},{8,10},{9,11},{10,... | collective-permute-start | bytes 786440 | tf_op jit(solution)/shard_map/ppermute | solution.py:13
  41.1 20.9 %collective-permute-start.22 = (bf16[64,2048]{1,0:T(8,128)(2,1)S(1)}, bf16[64,2048]{1,0:T(8,128)(2,1)S(1)}, u32[]{:S(2)}, u32[]{:S(2)}) collective-permute-start(bf16[64,2048]{1,0:T(8,128)(2,1)S(1)} %collective-permute-done.18.refs_0_), channel_id=1, source_target_pairs={{0,4},{1,5},{2,6},{3,7},{4,0},{5,1},{6,2},{7,3},{8,12},{9,13},{10,... | collective-permute-start | bytes 786440 | tf_op jit(solution)/shard_map/ppermute | solution.py:13
  42.4 19.7 %collective-permute-start.24 = (bf16[64,2048]{1,0:T(8,128)(2,1)S(1)}, bf16[64,2048]{1,0:T(8,128)(2,1)S(1)}, u32[]{:S(2)}, u32[]{:S(2)}) collective-permute-start(bf16[64,2048]{1,0:T(8,128)(2,1)S(1)} %collective-permute-done.18.refs_0_), channel_id=1, source_target_pairs={{0,6},{1,7},{2,4},{3,5},{4,2},{5,3},{6,0},{7,1},{8,14},{9,15},{10,... | collective-permute-start | bytes 786440 | tf_op jit(solution)/shard_map/ppermute | solution.py:13
  43.8 17.5 %collective-permute-start.17 = (s32[1,128]{1,0:T(1,128)S(1)}, s32[1,128]{1,0:T(1,128)S(1)}, u32[]{:S(2)}, u32[]{:S(2)}) collective-permute-start(s32[1,128]{1,0:T(1,128)S(1)} %dynamic-slice_bitcast_fusion.picks_ref), channel_id=1, source_target_pairs={{0,16},{8,24},{16,0},{24,8},{1,17},{9,25},{17,1},{25,9},{2,18},{10... | collective-permute-start | bytes 1544 | tf_op jit(solution)/shard_map/ppermute | solution.py:13
  60.1 9.9 %collective-permute-start.19 = (bf16[64,2048]{1,0:T(8,128)(2,1)S(1)}, bf16[64,2048]{1,0:T(8,128)(2,1)S(1)}, u32[]{:S(2)}, u32[]{:S(2)}) collective-permute-start(bf16[64,2048]{1,0:T(8,128)(2,1)S(1)} %collective-permute-done.18.refs_0_), channel_id=1, source_target_pairs={{0,1},{1,0},{2,3},{3,2},{4,5},{5,4},{6,7},{7,6},{8,9},{9,8},{10,11... | collective-permute-start | bytes 786440 | tf_op jit(solution)/shard_map/ppermute | solution.py:13
  61.3 17.6 %collective-permute-start.26 = (bf16[128,2048]{1,0:T(8,128)(2,1)S(1)}, bf16[128,2048]{1,0:T(8,128)(2,1)S(1)}, u32[]{:S(2)}, u32[]{:S(2)}) collective-permute-start(bf16[128,2048]{1,0:T(8,128)(2,1)S(1)} %select.3.refs_0_), channel_id=1, source_target_pairs={{0,8},{8,0},{16,24},{24,16},{1,9},{9,1},{17,25},{25,17},{2,10},{10... | collective-permute-start | bytes 1572872 | tf_op jit(solution)/shard_map/ppermute | solution.py:13
  61.4 15.4 %collective-permute-start.21 = (bf16[64,2048]{1,0:T(8,128)(2,1)S(1)}, bf16[64,2048]{1,0:T(8,128)(2,1)S(1)}, u32[]{:S(2)}, u32[]{:S(2)}) collective-permute-start(bf16[64,2048]{1,0:T(8,128)(2,1)S(1)} %collective-permute-done.20.refs_2_), channel_id=1, source_target_pairs={{0,1},{1,0},{2,3},{3,2},{4,5},{5,4},{6,7},{7,6},{8,9},{9,8},{10,11... | collective-permute-start | bytes 786440 | tf_op jit(solution)/shard_map/ppermute | solution.py:13
  62.0 15.7 %collective-permute-start.23 = (bf16[64,2048]{1,0:T(8,128)(2,1)S(1)}, bf16[64,2048]{1,0:T(8,128)(2,1)S(1)}, u32[]{:S(2)}, u32[]{:S(2)}) collective-permute-start(bf16[64,2048]{1,0:T(8,128)(2,1)S(1)} %collective-permute-done.22.refs_4_), channel_id=1, source_target_pairs={{0,1},{1,0},{2,3},{3,2},{4,5},{5,4},{6,7},{7,6},{8,9},{9,8},{10,11... | collective-permute-start | bytes 786440 | tf_op jit(solution)/shard_map/ppermute | solution.py:13
  62.1 15.7 %collective-permute-start.25 = (bf16[64,2048]{1,0:T(8,128)(2,1)S(1)}, bf16[64,2048]{1,0:T(8,128)(2,1)S(1)}, u32[]{:S(2)}, u32[]{:S(2)}) collective-permute-start(bf16[64,2048]{1,0:T(8,128)(2,1)S(1)} %collective-permute-done.24.refs_6_), channel_id=1, source_target_pairs={{0,1},{1,0},{2,3},{3,2},{4,5},{5,4},{6,7},{7,6},{8,9},{9,8},{10,11... | collective-permute-start | bytes 786440 | tf_op jit(solution)/shard_map/ppermute | solution.py:13
  69.9 19.5 %collective-permute-start.27 = (bf16[128,2048]{1,0:T(8,128)(2,1)S(1)}, bf16[128,2048]{1,0:T(8,128)(2,1)S(1)}, u32[]{:S(2)}, u32[]{:S(2)}) collective-permute-start(bf16[128,2048]{1,0:T(8,128)(2,1)S(1)} %get-tuple-element.22), channel_id=1, source_target_pairs={{0,8},{24,16},{1,9},{25,17},{2,10},{26,18},{3,11},{27,19},{4,12},{... | collective-permute-start | bytes 1572872 | tf_op jit(solution)/shard_map/ppermute | solution.py:13
  76.8 24.6 %collective-permute-start.16 = (bf16[128,2048]{1,0:T(8,128)(2,1)S(1)}, bf16[128,2048]{1,0:T(8,128)(2,1)S(1)}, u32[]{:S(2)}, u32[]{:S(2)}) collective-permute-start(bf16[128,2048]{1,0:T(8,128)(2,1)S(1)} %get-tuple-element.22), channel_id=1, source_target_pairs={{8,16},{16,8},{9,17},{17,9},{10,18},{18,10},{11,19},{19,11},{12,20... | collective-permute-start | bytes 1572872 | tf_op jit(solution)/shard_map/ppermute | solution.py:13
  86.4 51.6 %copy-start.4 = (bf16[64,2048]{1,0:T(8,128)(2,1)S(1)}, bf16[64,2048]{1,0:T(8,128)(2,1)}, u32[]{:S(2)}) copy-start(bf16[64,2048]{1,0:T(8,128)(2,1)} %refs_0_.3) | copy-start | bytes 786436
  86.4 15.0 %collective-permute-start.29 = (bf16[128,1024]{1,0:T(8,128)(2,1)S(1)}, bf16[128,1024]{1,0:T(8,128)(2,1)S(1)}, u32[]{:S(2)}, u32[]{:S(2)}) collective-permute-start(bf16[128,1024]{1,0:T(8,128)(2,1)S(1)} %get-tuple-element.24), channel_id=1, source_target_pairs={{0,8},{8,0},{16,24},{24,16},{1,9},{9,1},{17,25},{25,17},{2,10},{10... | collective-permute-start | bytes 786440 | tf_op jit(solution)/shard_map/ppermute | solution.py:13
  89.6 22.5 %collective-permute-start.28 = (bf16[128,1024]{1,0:T(8,128)(2,1)S(1)}, bf16[128,1024]{1,0:T(8,128)(2,1)S(1)}, u32[]{:S(2)}, u32[]{:S(2)}) collective-permute-start(bf16[128,1024]{1,0:T(8,128)(2,1)S(1)} %get-tuple-element.37), channel_id=1, source_target_pairs={{0,16},{8,24},{16,0},{24,8},{1,17},{9,25},{17,1},{25,9},{2,18},{10... | collective-permute-start | bytes 786440 | tf_op jit(solution)/shard_map/ppermute | solution.py:13
  93.7 22.1 %collective-permute-start.30 = (bf16[128,1024]{1,0:T(8,128)(2,1)S(1)}, bf16[128,1024]{1,0:T(8,128)(2,1)S(1)}, u32[]{:S(2)}, u32[]{:S(2)}) collective-permute-start(bf16[128,1024]{1,0:T(8,128)(2,1)S(1)} %get-tuple-element.36), channel_id=1, source_target_pairs={{0,16},{8,24},{16,0},{24,8},{1,17},{9,25},{17,1},{25,9},{2,18},{10... | collective-permute-start | bytes 786440 | tf_op jit(solution)/shard_map/ppermute | solution.py:13
  93.8 22.7 %collective-permute-start.31 = (bf16[128,1024]{1,0:T(8,128)(2,1)S(1)}, bf16[128,1024]{1,0:T(8,128)(2,1)S(1)}, u32[]{:S(2)}, u32[]{:S(2)}) collective-permute-start(bf16[128,1024]{1,0:T(8,128)(2,1)S(1)} %get-tuple-element.29), channel_id=1, source_target_pairs={{0,8},{8,0},{16,24},{24,16},{1,9},{9,1},{17,25},{25,17},{2,10},{10... | collective-permute-start | bytes 786440 | tf_op jit(solution)/shard_map/ppermute | solution.py:13
  112.3 6.4 %collective-permute-start.40 = (bf16[128,1024]{1,0:T(8,128)(2,1)S(1)}, bf16[128,1024]{1,0:T(8,128)(2,1)S(1)}, u32[]{:S(2)}, u32[]{:S(2)}) collective-permute-start(bf16[128,1024]{1,0:T(8,128)(2,1)S(1)} %add_convert_fusion.2.refs_5_), channel_id=1, source_target_pairs={{0,2},{1,3},{2,0},{3,1},{4,6},{5,7},{6,4},{7,5},{8,10},{9,11},{10,... | collective-permute-start | bytes 786440 | tf_op jit(solution)/shard_map/ppermute | solution.py:13
  113.0 8.1 %collective-permute-start.42 = (bf16[128,1024]{1,0:T(8,128)(2,1)S(1)}, bf16[128,1024]{1,0:T(8,128)(2,1)S(1)}, u32[]{:S(2)}, u32[]{:S(2)}) collective-permute-start(bf16[128,1024]{1,0:T(8,128)(2,1)S(1)} %add_convert_fusion.2.refs_5_), channel_id=1, source_target_pairs={{0,4},{1,5},{2,6},{3,7},{4,0},{5,1},{6,2},{7,3},{8,12},{9,13},{10,... | collective-permute-start | bytes 786440 | tf_op jit(solution)/shard_map/ppermute | solution.py:13
  114.4 11.1 %collective-permute-start.44 = (bf16[128,1024]{1,0:T(8,128)(2,1)S(1)}, bf16[128,1024]{1,0:T(8,128)(2,1)}, u32[]{:S(2)}, u32[]{:S(2)}) collective-permute-start(bf16[128,1024]{1,0:T(8,128)(2,1)S(1)} %add_convert_fusion.2.refs_5_), channel_id=1, source_target_pairs={{0,6},{1,7},{2,4},{3,5},{4,2},{5,3},{6,0},{7,1},{8,14},{9,15},{10,... | collective-permute-start | bytes 786440 | tf_op jit(solution)/shard_map/ppermute | solution.py:13
  115.8 10.4 %collective-permute-start.39 = (bf16[128,1024]{1,0:T(8,128)(2,1)S(1)}, bf16[128,1024]{1,0:T(8,128)(2,1)S(1)}, u32[]{:S(2)}, u32[]{:S(2)}) collective-permute-start(bf16[128,1024]{1,0:T(8,128)(2,1)S(1)} %add_convert_fusion.2.refs_5_), channel_id=1, source_target_pairs={{0,1},{1,0},{2,3},{3,2},{4,5},{5,4},{6,7},{7,6},{8,9},{9,8},{10,11... | collective-permute-start | bytes 786440 | tf_op jit(solution)/shard_map/ppermute | solution.py:13
  117.4 10.7 %collective-permute-start.33 = (bf16[128,1024]{1,0:T(8,128)(2,1)}, bf16[128,1024]{1,0:T(8,128)(2,1)}, u32[]{:S(2)}, u32[]{:S(2)}) collective-permute-start(bf16[128,1024]{1,0:T(8,128)(2,1)} %add_convert_fusion.refs_5_), channel_id=1, source_target_pairs={{0,2},{1,3},{2,0},{3,1},{4,6},{5,7},{6,4},{7,5},{8,10},{9,11},{10,... | collective-permute-start | bytes 786440 | tf_op jit(solution)/shard_map/ppermute | solution.py:13
  118.7 13.8 %collective-permute-start.35 = (bf16[128,1024]{1,0:T(8,128)(2,1)}, bf16[128,1024]{1,0:T(8,128)(2,1)}, u32[]{:S(2)}, u32[]{:S(2)}) collective-permute-start(bf16[128,1024]{1,0:T(8,128)(2,1)} %add_convert_fusion.refs_5_), channel_id=1, source_target_pairs={{0,4},{1,5},{2,6},{3,7},{4,0},{5,1},{6,2},{7,3},{8,12},{9,13},{10,... | collective-permute-start | bytes 786440 | tf_op jit(solution)/shard_map/ppermute | solution.py:13
  121.1 12.7 %collective-permute-start.37 = (bf16[128,1024]{1,0:T(8,128)(2,1)}, bf16[128,1024]{1,0:T(8,128)(2,1)}, u32[]{:S(2)}, u32[]{:S(2)}) collective-permute-start(bf16[128,1024]{1,0:T(8,128)(2,1)} %add_convert_fusion.refs_5_), channel_id=1, source_target_pairs={{0,6},{1,7},{2,4},{3,5},{4,2},{5,3},{6,0},{7,1},{8,14},{9,15},{10,... | collective-permute-start | bytes 786440 | tf_op jit(solution)/shard_map/ppermute | solution.py:13
  125.5 8.3 %collective-permute-start.41 = (bf16[128,1024]{1,0:T(8,128)(2,1)S(1)}, bf16[128,1024]{1,0:T(8,128)(2,1)S(1)}, u32[]{:S(2)}, u32[]{:S(2)}) collective-permute-start(bf16[128,1024]{1,0:T(8,128)(2,1)S(1)} %collective-permute-done.40.refs_7_), channel_id=1, source_target_pairs={{0,1},{1,0},{2,3},{3,2},{4,5},{5,4},{6,7},{7,6},{8,9},{9,8},{10,11... | collective-permute-start | bytes 786440 | tf_op jit(solution)/shard_map/ppermute | solution.py:13
  126.9 8.1 %collective-permute-start.43 = (bf16[128,1024]{1,0:T(8,128)(2,1)S(1)}, bf16[128,1024]{1,0:T(8,128)(2,1)S(1)}, u32[]{:S(2)}, u32[]{:S(2)}) collective-permute-start(bf16[128,1024]{1,0:T(8,128)(2,1)S(1)} %collective-permute-done.42.refs_9_), channel_id=1, source_target_pairs={{0,1},{1,0},{2,3},{3,2},{4,5},{5,4},{6,7},{7,6},{8,9},{9,8},{10,11... | collective-permute-start | bytes 786440 | tf_op jit(solution)/shard_map/ppermute | solution.py:13
  128.1 19.8 %collective-permute-start.45 = (bf16[128,1024]{1,0:T(8,128)(2,1)}, bf16[128,1024]{1,0:T(8,128)(2,1)}, u32[]{:S(2)}, u32[]{:S(2)}) collective-permute-start(bf16[128,1024]{1,0:T(8,128)(2,1)} %collective-permute-done.44.refs_11_), channel_id=1, source_target_pairs={{0,1},{1,0},{2,3},{3,2},{4,5},{5,4},{6,7},{7,6},{8,9},{9,8},{10,11... | collective-permute-start | bytes 786440 | tf_op jit(solution)/shard_map/ppermute | solution.py:13
  132.5 25.0 %collective-permute-start.32 = (bf16[128,1024]{1,0:T(8,128)(2,1)}, bf16[128,1024]{1,0:T(8,128)(2,1)}, u32[]{:S(2)}, u32[]{:S(2)}) collective-permute-start(bf16[128,1024]{1,0:T(8,128)(2,1)} %add_convert_fusion.refs_5_), channel_id=1, source_target_pairs={{0,1},{1,0},{2,3},{3,2},{4,5},{5,4},{6,7},{7,6},{8,9},{9,8},{10,11... | collective-permute-start | bytes 786440 | tf_op jit(solution)/shard_map/ppermute | solution.py:13
  133.8 23.6 %collective-permute-start.34 = (bf16[128,1024]{1,0:T(8,128)(2,1)}, bf16[128,1024]{1,0:T(8,128)(2,1)}, u32[]{:S(2)}, u32[]{:S(2)}) collective-permute-start(bf16[128,1024]{1,0:T(8,128)(2,1)} %collective-permute-done.33.refs_7_), channel_id=1, source_target_pairs={{0,1},{1,0},{2,3},{3,2},{4,5},{5,4},{6,7},{7,6},{8,9},{9,8},{10,11... | collective-permute-start | bytes 786440 | tf_op jit(solution)/shard_map/ppermute | solution.py:13
  134.5 22.9 %collective-permute-start.36 = (bf16[128,1024]{1,0:T(8,128)(2,1)}, bf16[128,1024]{1,0:T(8,128)(2,1)}, u32[]{:S(2)}, u32[]{:S(2)}) collective-permute-start(bf16[128,1024]{1,0:T(8,128)(2,1)} %collective-permute-done.35.refs_9_), channel_id=1, source_target_pairs={{0,1},{1,0},{2,3},{3,2},{4,5},{5,4},{6,7},{7,6},{8,9},{9,8},{10,11... | collective-permute-start | bytes 786440 | tf_op jit(solution)/shard_map/ppermute | solution.py:13
  135.7 21.7 %collective-permute-start.38 = (bf16[128,1024]{1,0:T(8,128)(2,1)}, bf16[128,1024]{1,0:T(8,128)(2,1)}, u32[]{:S(2)}, u32[]{:S(2)}) collective-permute-start(bf16[128,1024]{1,0:T(8,128)(2,1)} %collective-permute-done.37.refs_11_), channel_id=1, source_target_pairs={{0,1},{1,0},{2,3},{3,2},{4,5},{5,4},{6,7},{7,6},{8,9},{9,8},{10,11... | collective-permute-start | bytes 786440 | tf_op jit(solution)/shard_map/ppermute | solution.py:13
  (31 other events, 396.5 us)
